TPU v7x, 32 devices: a whole 2x2x4 slice. The times are simulated.
32 devices in a mesh: row: 4 (over x, core), col: 8 (over z, y).
Axes of the slice: x: 2, y: 2, z: 4, core: 2. Of those that a mesh axis runs over, the one named last changes fastest.
Arguments:
- right_sides: bfloat16 [1024, 64, 128], P(('row', 'col')), may hold values from -7 to 7
- weights_fine: bfloat16 [1024, 3, 128, 128], P(('row', 'col')), may hold values from 0 to 2
- columns_fine: int32 [1024, 3], P(('row', 'col')), may hold values from 0 to 1023, as said below
- degree_fine: float32 [1024, 128], P(('row', 'col')), may hold values from 0.05 to 0.5
- owners_fine: int32 [1024, 128], P(('row', 'col')), may hold values from 0 to 31, as said below
- slots_fine: int32 [1024, 128], P(('row', 'col')), may hold values from 0 to 1023
- weights_second: bfloat16 [256, 3, 128, 128], P(('row', 'col')), may hold values from 0 to 8
- columns_second: int32 [256, 3], P(('row', 'col')), may hold values from 0 to 255, as said below
- degree_second: float32 [256, 128], P(('row', 'col')), may hold values from 0.2 to 2
- owners_second: int32 [256, 128], P(('row', 'col')), may hold values from 0 to 31, as said below
- slots_second: int32 [256, 128], P(('row', 'col')), may hold values from 0 to 255
- weights_third: bfloat16 [64, 3, 128, 128], P(('row', 'col')), may hold values from 0 to 32
- columns_third: int32 [64, 3], P(('row', 'col')), may hold values from 0 to 63, as said below
- degree_third: float32 [64, 128], P(('row', 'col')), may hold values from 0.8 to 8
- owners_third: int32 [64, 128], P(('row', 'col')), may hold values from 0 to 31, as said below
- slots_third: int32 [64, 128], P(('row', 'col')), may hold values from 0 to 127
- coarse_inverse: bfloat16 [4096, 1024], P(('row', 'col')), may hold values from -1 to 1, as said below
Outputs:
- solution: float32 [1024, 64, 128], P(('row', 'col'))
Inputs may be any that keep to these rules, and one draw needn't show every extreme that they name: `columns_fine`: every entry lies within 2 blocks of its own row block's index, on the same level. `columns_second`: every entry lies within 2 blocks of its own row block's index, on the same level. `columns_third`: every entry lies within 2 blocks of its own row block's index, on the same level. `owners_fine`: each entry is the device holding the vertex or the one just before or after it in device order. `owners_second`: each entry is the device holding the vertex or the one just before or after it in device order. `owners_third`: each entry is the device holding the vertex or the one just before or after it in device order. `coarse_inverse`: each row group's block is symmetric.
All inputs are finite; a program needn't handle non-finite values.
Results may differ from a plain program's by a relative error of at most 0.0003.
Values may be sent and summed in bfloat16 or wider, within the bound.
A program may use at most 64 MiB of HBM per device.

v0:
```python
import jax
import jax.numpy as jnp
from jax import lax
from jax.sharding import PartitionSpec as P

BS = 128
K = 3
HB = 2
SWEEPS = 2
NB2 = 2
NB1 = 8
C3 = 128


damping = 0.8


def extended_2(block, sides, width):
    for axis, dim in sides:
        count = lax.axis_size(axis)
        forward = [(i, i + 1) for i in range(count - 1)]
        backward = [(target, source) for source, target in forward]
        low = lax.ppermute(
            lax.slice_in_dim(block, block.shape[dim] - width, None, axis=dim), axis, forward
        )
        high = lax.ppermute(lax.slice_in_dim(block, 0, width, axis=dim), axis, backward)
        block = jnp.concatenate([low, block, high], axis=dim)
    return block


def as_sent(x):
    return jax.tree.map(lambda a: a.astype(jnp.bfloat16) if a.dtype == jnp.float32 else a, x)


def passed_along(value, axis, steps):
    count = lax.axis_size(axis)
    initial, last = (max(0, -steps), min(count, count - steps))
    return lax.ppermute(value, axis, [(source, source + steps) for source in range(initial, last)])


def gather_rows(blocks):
    return jnp.transpose(blocks, (0, 2, 1)).reshape(-1, blocks.shape[1])


def make_blocks(rows_data):
    return jnp.transpose(rows_data.reshape(-1, BS, rows_data.shape[1]), (0, 2, 1))


def complete_diagonal_entries(weights, shift):
    return shift + jnp.sum(weights, axis=(1, 2), dtype=jnp.float32) / (K * BS)


def apply_operator(current_iterate, weights, columns, degree, device):
    block_total_number = current_iterate.shape[0]
    rounded = current_iterate.astype(jnp.bfloat16)
    extended = extended_2(rounded, ((("row", "col"), 0),), HB)
    offset = device * block_total_number - HB
    picked = extended[columns - offset]
    product = jnp.einsum("nkrb,nkbc->nrc", picked, weights, preferred_element_type=jnp.float32)
    return degree[:, None, :] * current_iterate - product / (K * BS)


def restrict(residual, aggregate_owners, slots, coarse_count, device):
    targets = ((aggregate_owners - device + 1) * coarse_count + slots).reshape(-1)
    partial_value = jax.ops.segment_sum(
        gather_rows(residual), targets, num_segments=3 * coarse_count
    )
    upward = passed_along(as_sent(partial_value[2 * coarse_count :]), ("row", "col"), 1)
    downward = passed_along(as_sent(partial_value[:coarse_count]), ("row", "col"), -1)
    return partial_value[coarse_count : 2 * coarse_count] + upward + downward


def prolong(current_iterate, coarse_correction_rows, aggregate_owners, slots, coarse_count, device):
    extended = extended_2(
        as_sent(coarse_correction_rows), ((("row", "col"), 0),), coarse_count
    ).astype(coarse_correction_rows.dtype)
    targets = ((aggregate_owners - device + 1) * coarse_count + slots).reshape(-1)
    return current_iterate + make_blocks(extended[targets])


def coarse_solve(coarse_rows, coarse_inverse):
    rounded = jnp.transpose(coarse_rows).astype(jnp.bfloat16)
    solved = lax.dot_general(
        lax.all_gather(rounded, "col", axis=1, tiled=True),
        coarse_inverse,
        (((1,), (1,)), ((), ())),
        preferred_element_type=jnp.float32,
    )
    return jnp.transpose(solved)


def on_device(
    right_sides,
    weights_fine,
    columns_fine,
    degree_fine,
    owners_fine,
    slots_fine,
    weights_second,
    columns_second,
    degree_second,
    owners_second,
    slots_second,
    weights_third,
    columns_third,
    degree_third,
    owners_third,
    slots_third,
    coarse_inverse,
):
    device = lax.axis_index(("row", "col"))
    levels = [
        (
            weights_fine,
            columns_fine,
            complete_diagonal_entries(weights_fine, degree_fine),
            owners_fine,
            slots_fine,
            NB1 * BS,
        ),
        (
            weights_second,
            columns_second,
            complete_diagonal_entries(weights_second, degree_second),
            owners_second,
            slots_second,
            NB2 * BS,
        ),
        (
            weights_third,
            columns_third,
            complete_diagonal_entries(weights_third, degree_third),
            owners_third,
            slots_third,
            C3,
        ),
    ]
    source = right_sides.astype(jnp.float32)
    stored = []
    coarse_rows = None
    for position in range(3):
        weights, columns, degree, aggregate_owners, slots, coarse_count = levels[position]
        scale = degree[:, None, :]
        current_iterate = damping * source / scale
        current_iterate = (
            current_iterate
            + damping
            * (source - apply_operator(current_iterate, weights, columns, degree, device))
            / scale
        )
        residual = source - apply_operator(current_iterate, weights, columns, degree, device)
        stored.append((current_iterate, source))
        coarse_rows = restrict(residual, aggregate_owners, slots, coarse_count, device)
        if position < 2:
            source = make_blocks(coarse_rows)
    coarse_correction_rows = coarse_solve(coarse_rows, coarse_inverse)
    current_iterate = None
    for position in (2, 1, 0):
        weights, columns, degree, aggregate_owners, slots, coarse_count = levels[position]
        current_iterate, source = stored[position]
        current_iterate = prolong(
            current_iterate, coarse_correction_rows, aggregate_owners, slots, coarse_count, device
        )
        scale = degree[:, None, :]
        for repeat in range(SWEEPS):
            current_iterate = (
                current_iterate
                + damping
                * (source - apply_operator(current_iterate, weights, columns, degree, device))
                / scale
            )
        coarse_correction_rows = gather_rows(current_iterate)
    return current_iterate


def solution(mesh):
    in_specs = (
        P(("row", "col"), None, None),
        P(("row", "col"), None, None, None),
        P(("row", "col"), None),
        P(("row", "col"), None),
        P(("row", "col"), None),
        P(("row", "col"), None),
        P(("row", "col"), None, None, None),
        P(("row", "col"), None),
        P(("row", "col"), None),
        P(("row", "col"), None),
        P(("row", "col"), None),
        P(("row", "col"), None, None, None),
        P(("row", "col"), None),
        P(("row", "col"), None),
        P(("row", "col"), None),
        P(("row", "col"), None),
        P(("row", "col"), None),
    )
    out_specs = P(("row", "col"), None, None)
    return jax.shard_map(
        on_device, mesh=mesh, in_specs=in_specs, out_specs=out_specs, check_vma=False
    )
```

profile of v0, /device:TPU:2, one launch (start us, length us, event | category | flops | bytes accessed | tf_op | source)
XLA Modules:
  0.0 333.1 jit_solution(1003696899687484927)
XLA Ops:
  0.0 2.6 convert_reduce_fusion
  2.9 3.4 %collective-permute-start = (bf16[2,64,128]{2,1,0:T(8,128)(2,1)S(1)}, bf16[2,64,128]{2,1,0:T(8,128)(2,1)S(1)}, u32[]{:S(2)}, u32[]{:S(2)}) collective-permute-start(bf16[2,64,128]{2,1,0:T(8,128)(2,1)S(1)} %get-tuple-element.17), channel_id=1, source_target_pairs={{0,1},{1,2},{2,3},{3,4},{4,5},{5,6},{6,7},{7,8},{8,9},{9,10},{10,1... | collective-permute-start | bytes 98312 | tf_op jit(solution)/shard_map/ppermute | solution.py:23
  6.3 5.7 %collective-permute-start.1 = (bf16[2,64,128]{2,1,0:T(8,128)(2,1)S(1)}, bf16[2,64,128]{2,1,0:T(8,128)(2,1)S(1)}, u32[]{:S(2)}, u32[]{:S(2)}) collective-permute-start(bf16[2,64,128]{2,1,0:T(8,128)(2,1)S(1)} %get-tuple-element.18), channel_id=1, source_target_pairs={{1,0},{2,1},{3,2},{4,3},{5,4},{6,5},{7,6},{8,7},{9,8},{10,9},{11,1... | collective-permute-start | bytes 98312 | tf_op jit(solution)/shard_map/ppermute | solution.py:26
  14.5 3.2 gather_fusion
  17.7 3.3 %fusion.112 = (bf16[32,64,128]{2,1,0:T(8,128)(2,1)S(1)}, f32[32,64,128]{2,1,0:T(8,128)}) fusion(bf16[32,3,64,128]{3,2,1,0:T(8,128)(2,1)} %bitcast.366, bf16[32,3,128,128]{3,2,1,0:T(8,128)(2,1)S(1)} %copy-done.1, f32[32,128]{1,0:T(8,128)S(1)} %multiply_add_fusion.1, bf16[32,64,128]{2,1,0:T(8,128)(2,1)} %param.17), kind=kOutput, calls=%fused_computation.198 | convolution fusion | flops 204210176 | bytes 6832128 | tf_op jit(solution)/shard_map/nkrb,nkbc->nrc/dot_general | solution.py:59
  22.4 2.8 collective-permute-start.2
  25.3 6.3 %collective-permute-start.3 = (bf16[2,64,128]{2,1,0:T(8,128)(2,1)S(1)}, bf16[2,64,128]{2,1,0:T(8,128)(2,1)S(1)}, u32[]{:S(2)}, u32[]{:S(2)}) collective-permute-start(bf16[2,64,128]{2,1,0:T(8,128)(2,1)S(1)} %get-tuple-element.16), channel_id=1, source_target_pairs={{1,0},{2,1},{3,2},{4,3},{5,4},{6,5},{7,6},{8,7},{9,8},{10,9},{11,1... | collective-permute-start | bytes 98312 | tf_op jit(solution)/shard_map/ppermute | solution.py:26
  33.2 1.9 pad_maximum_fusion.1
  35.1 3.0 gather_fusion.1
  38.2 3.6 %fusion.6 = f32[32,128,64]{1,2,0:T(8,128)} fusion(bf16[32,3,64,128]{3,2,1,0:T(8,128)(2,1)} %bitcast.360, bf16[32,3,128,128]{3,2,1,0:T(8,128)(2,1)S(1)} %copy-done.1, bf16[32,64,128]{2,1,0:T(8,128)(2,1)} %param.17, f32[32,64,128]{2,1,0:T(8,128)} %get-tuple-element.32, f32[32,128]{1,0:T(8,128)S(1)} %multiply_add_fusion.1), kind=kOutput, calls=%fused_computation.34 | convolution fusion | flops 202637312 | bytes 7356416 | tf_op jit(solution)/shard_map/nkrb,nkbc->nrc/dot_general | solution.py:59
  41.8 3.2 copy.106
  45.0 23.0 %scatter_custom_fusion = f32[3072,64]{1,0:T(8,128)S(1)} fusion(s32[4096]{0:T(1024)S(1)} %bitcast.385, f32[4096,64]{1,0:T(8,128)} %bitcast.362, f32[]{:T(128)} %constant.22.clone.1), kind=kCustom, calls=%fused_computation.89 | custom fusion | flops 262144 | bytes 786944 | tf_op jit(solution)/shard_map/scatter-add | solution.py:65
  68.2 1.9 collective-permute-start.4
  70.1 7.2 %collective-permute-start.5 = (bf16[1024,64]{1,0:T(8,128)(2,1)S(1)}, bf16[1024,64]{1,0:T(8,128)(2,1)}, u32[]{:S(2)}, u32[]{:S(2)}) collective-permute-start(bf16[1024,64]{1,0:T(8,128)(2,1)S(1)} %get-tuple-element.10), channel_id=1, source_target_pairs={{1,0},{2,1},{3,2},{4,3},{5,4},{6,5},{7,6},{8,7},{9,8},{10,9},{11,1... | collective-permute-start | bytes 393224 | tf_op jit(solution)/shard_map/ppermute | solution.py:38
  77.6 2.5 collective-permute-done.4
  80.1 3.7 %collective-permute-done.5 = bf16[1024,64]{1,0:T(8,128)(2,1)} collective-permute-done((bf16[1024,64]{1,0:T(8,128)(2,1)S(1)}, bf16[1024,64]{1,0:T(8,128)(2,1)}, u32[]{:S(2)}, u32[]{:S(2)}) %collective-permute-start.5) | collective-permute-done | bytes 131104 | tf_op jit(solution)/shard_map/ppermute | solution.py:38
  85.1 1.9 collective-permute-start.6
  87.0 7.2 %collective-permute-start.7 = (bf16[2,64,128]{2,1,0:T(8,128)(2,1)S(1)}, bf16[2,64,128]{2,1,0:T(8,128)(2,1)S(1)}, u32[]{:S(2)}, u32[]{:S(2)}) collective-permute-start(bf16[2,64,128]{2,1,0:T(8,128)(2,1)S(1)} %get-tuple-element.28), channel_id=1, source_target_pairs={{1,0},{2,1},{3,2},{4,3},{5,4},{6,5},{7,6},{8,7},{9,8},{10,9},{11,1... | collective-permute-start | bytes 98312 | tf_op jit(solution)/shard_map/ppermute | solution.py:26
  96.8 1.9 collective-permute-start.8
  98.8 7.2 %collective-permute-start.9 = (bf16[2,64,128]{2,1,0:T(8,128)(2,1)S(1)}, bf16[2,64,128]{2,1,0:T(8,128)(2,1)S(1)}, u32[]{:S(2)}, u32[]{:S(2)}) collective-permute-start(bf16[2,64,128]{2,1,0:T(8,128)(2,1)S(1)} %get-tuple-element.26), channel_id=1, source_target_pairs={{1,0},{2,1},{3,2},{4,3},{5,4},{6,5},{7,6},{8,7},{9,8},{10,9},{11,1... | collective-permute-start | bytes 98312 | tf_op jit(solution)/shard_map/ppermute | solution.py:26
  108.8 6.1 %scatter_custom_fusion.1 = f32[768,64]{1,0:T(8,128)S(1)} fusion(s32[1024]{0:T(1024)S(1)} %bitcast.388, f32[1024,64]{1,0:T(8,128)S(1)} %bitcast.372, f32[]{:T(128)} %constant.22.clone.1), kind=kCustom, calls=%fused_computation.127 | custom fusion | flops 65536 | bytes 196612 | tf_op jit(solution)/shard_map/scatter-add | solution.py:65
  115.0 1.9 collective-permute-start.10
  116.9 7.2 %collective-permute-start.11 = (bf16[256,64]{1,0:T(8,128)(2,1)S(1)}, bf16[256,64]{1,0:T(8,128)(2,1)S(1)}, u32[]{:S(2)}, u32[]{:S(2)}) collective-permute-start(bf16[256,64]{1,0:T(8,128)(2,1)S(1)} %get-tuple-element.20), channel_id=1, source_target_pairs={{1,0},{2,1},{3,2},{4,3},{5,4},{6,5},{7,6},{8,7},{9,8},{10,9},{11,1... | collective-permute-start | bytes 98312 | tf_op jit(solution)/shard_map/ppermute | solution.py:38
  124.3 1.8 collective-permute-done.11
  126.2 1.9 collective-permute-start.12
  128.1 7.3 %collective-permute-start.13 = (bf16[2,64,128]{2,1,0:T(8,128)(2,1)S(1)}, bf16[2,64,128]{2,1,0:T(8,128)(2,1)S(1)}, u32[]{:S(2)}, u32[]{:S(2)}) collective-permute-start(bf16[2,64,128]{2,1,0:T(8,128)(2,1)S(1)} %fusion.94), channel_id=1, source_target_pairs={{1,0},{2,1},{3,2},{4,3},{5,4},{6,5},{7,6},{8,7},{9,8},{10,9},{11,1... | collective-permute-start | bytes 98312 | tf_op jit(solution)/shard_map/ppermute | solution.py:26
  137.7 1.9 collective-permute-start.14
  139.7 7.2 %collective-permute-start.15 = (bf16[2,64,128]{2,1,0:T(8,128)(2,1)S(1)}, bf16[2,64,128]{2,1,0:T(8,128)(2,1)S(1)}, u32[]{:S(2)}, u32[]{:S(2)}) collective-permute-start(bf16[2,64,128]{2,1,0:T(8,128)(2,1)S(1)} %get-tuple-element.5), channel_id=1, source_target_pairs={{1,0},{2,1},{3,2},{4,3},{5,4},{6,5},{7,6},{8,7},{9,8},{10,9},{11,1... | collective-permute-start | bytes 98312 | tf_op jit(solution)/shard_map/ppermute | solution.py:26
  149.4 1.7 scatter_custom_fusion.2
  151.1 1.9 collective-permute-start.16
  153.0 7.3 %collective-permute-start.17 = (bf16[128,64]{1,0:T(8,128)(2,1)S(1)}, bf16[128,64]{1,0:T(8,128)(2,1)S(1)}, u32[]{:S(2)}, u32[]{:S(2)}) collective-permute-start(bf16[128,64]{1,0:T(8,128)(2,1)S(1)} %get-tuple-element.30), channel_id=1, source_target_pairs={{1,0},{2,1},{3,2},{4,3},{5,4},{6,5},{7,6},{8,7},{9,8},{10,9},{11,1... | collective-permute-start | bytes 49160 | tf_op jit(solution)/shard_map/ppermute | solution.py:38
  162.0 30.8 %all_gather.3 = bf16[64,1024]{0,1:T(8,128)(2,1)S(1)} all-gather(bf16[64,128]{0,1:T(8,128)(2,1)S(1)} %fusion.95), channel_id=1, replica_groups=mesh['row'=4,'col'=8] {'col'}, dimensions={1}, use_global_device_ids=true | all-gather | bytes 147456 | tf_op jit(solution)/shard_map/all_gather | solution.py:84
  193.0 1.9 collective-permute-start.18
  194.9 7.2 %collective-permute-start.19 = (bf16[128,64]{0,1:T(8,128)(2,1)S(1)}, bf16[128,64]{0,1:T(8,128)(2,1)S(1)}, u32[]{:S(2)}, u32[]{:S(2)}) collective-permute-start(bf16[128,64]{0,1:T(8,128)(2,1)S(1)} %fusion.46), channel_id=1, source_target_pairs={{1,0},{2,1},{3,2},{4,3},{5,4},{6,5},{7,6},{8,7},{9,8},{10,9},{11,1... | collective-permute-start | bytes 49160 | tf_op jit(solution)/shard_map/ppermute | solution.py:26
  204.5 1.9 collective-permute-start.20
  206.5 7.2 %collective-permute-start.21 = (bf16[2,64,128]{2,1,0:T(8,128)(2,1)S(1)}, bf16[2,64,128]{2,1,0:T(8,128)(2,1)S(1)}, u32[]{:S(2)}, u32[]{:S(2)}) collective-permute-start(bf16[2,64,128]{2,1,0:T(8,128)(2,1)S(1)} %fusion.96), channel_id=1, source_target_pairs={{1,0},{2,1},{3,2},{4,3},{5,4},{6,5},{7,6},{8,7},{9,8},{10,9},{11,1... | collective-permute-start | bytes 98312 | tf_op jit(solution)/shard_map/ppermute | solution.py:26
  213.7 1.6 collective-permute-done.21
  216.1 1.9 collective-permute-start.22
  218.0 7.2 %collective-permute-start.23 = (bf16[2,64,128]{2,1,0:T(8,128)(2,1)S(1)}, bf16[2,64,128]{2,1,0:T(8,128)(2,1)S(1)}, u32[]{:S(2)}, u32[]{:S(2)}) collective-permute-start(bf16[2,64,128]{2,1,0:T(8,128)(2,1)S(1)} %get-tuple-element.35), channel_id=1, source_target_pairs={{1,0},{2,1},{3,2},{4,3},{5,4},{6,5},{7,6},{8,7},{9,8},{10,9},{11,1... | collective-permute-start | bytes 98312 | tf_op jit(solution)/shard_map/ppermute | solution.py:26
  227.7 1.9 collective-permute-start.24
  229.7 7.2 %collective-permute-start.25 = (bf16[256,64]{1,0:T(8,128)(2,1)S(1)}, bf16[256,64]{1,0:T(8,128)(2,1)S(1)}, u32[]{:S(2)}, u32[]{:S(2)}) collective-permute-start(bf16[256,64]{1,0:T(8,128)(2,1)S(1)} %bitcast.379), channel_id=1, source_target_pairs={{1,0},{2,1},{3,2},{4,3},{5,4},{6,5},{7,6},{8,7},{9,8},{10,9},{11,1... | collective-permute-start | bytes 98312 | tf_op jit(solution)/shard_map/ppermute | solution.py:26
  236.9 1.9 collective-permute-done.25
  238.8 2.8 gather_fusion.9
  241.9 1.9 collective-permute-start.26
  243.8 7.3 %collective-permute-start.27 = (bf16[2,64,128]{2,1,0:T(8,128)(2,1)S(1)}, bf16[2,64,128]{2,1,0:T(8,128)(2,1)S(1)}, u32[]{:S(2)}, u32[]{:S(2)}) collective-permute-start(bf16[2,64,128]{2,1,0:T(8,128)(2,1)S(1)} %get-tuple-element.24), channel_id=1, source_target_pairs={{1,0},{2,1},{3,2},{4,3},{5,4},{6,5},{7,6},{8,7},{9,8},{10,9},{11,1... | collective-permute-start | bytes 98312 | tf_op jit(solution)/shard_map/ppermute | solution.py:26
  251.1 1.6 collective-permute-done.27
  253.7 1.9 collective-permute-start.28
  255.6 7.2 %collective-permute-start.29 = (bf16[2,64,128]{2,1,0:T(8,128)(2,1)S(1)}, bf16[2,64,128]{2,1,0:T(8,128)(2,1)S(1)}, u32[]{:S(2)}, u32[]{:S(2)}) collective-permute-start(bf16[2,64,128]{2,1,0:T(8,128)(2,1)S(1)} %get-tuple-element.22), channel_id=1, source_target_pairs={{1,0},{2,1},{3,2},{4,3},{5,4},{6,5},{7,6},{8,7},{9,8},{10,9},{11,1... | collective-permute-start | bytes 98312 | tf_op jit(solution)/shard_map/ppermute | solution.py:26
  265.7 1.9 collective-permute-start.30
  267.6 7.6 %collective-permute-start.31 = (bf16[1024,64]{1,0:T(8,128)(2,1)S(1)}, bf16[1024,64]{1,0:T(8,128)(2,1)S(1)}, u32[]{:S(2)}, u32[]{:S(2)}) collective-permute-start(bf16[1024,64]{1,0:T(8,128)(2,1)S(1)} %bitcast.369), channel_id=1, source_target_pairs={{1,0},{2,1},{3,2},{4,3},{5,4},{6,5},{7,6},{8,7},{9,8},{10,9},{11,1... | collective-permute-start | bytes 393224 | tf_op jit(solution)/shard_map/ppermute | solution.py:26
  275.2 2.2 collective-permute-done.30
  277.4 1.7 collective-permute-done.31
  279.2 14.1 %gather_fusion.12 = f32[4096,64]{1,0:T(8,128)} fusion(f32[3072,64]{1,0:T(8,128)S(1)} %maximum_convert_fusion, s32[4096]{0:T(1024)S(1)} %broadcast_clamp_fusion), kind=kCustom, calls=%fused_computation.12 | custom fusion | bytes 2113536 | tf_op jit(solution)/shard_map/gather | solution.py:78
  293.3 2.3 copy.93
  295.8 1.9 collective-permute-start.32
  297.7 7.4 %collective-permute-start.33 = (bf16[2,64,128]{2,1,0:T(8,128)(2,1)S(1)}, bf16[2,64,128]{2,1,0:T(8,128)(2,1)S(1)}, u32[]{:S(2)}, u32[]{:S(2)}) collective-permute-start(bf16[2,64,128]{2,1,0:T(8,128)(2,1)S(1)} %get-tuple-element.14), channel_id=1, source_target_pairs={{1,0},{2,1},{3,2},{4,3},{5,4},{6,5},{7,6},{8,7},{9,8},{10,9},{11,1... | collective-permute-start | bytes 98312 | tf_op jit(solution)/shard_map/ppermute | solution.py:26
  305.1 1.6 collective-permute-done.33
  307.6 3.2 gather_fusion.13
  310.8 4.0 %fusion.113 = (bf16[32,64,128]{2,1,0:T(8,128)(2,1)S(1)}, f32[32,64,128]{2,1,0:T(8,128)}) fusion(bf16[32,3,64,128]{3,2,1,0:T(8,128)(2,1)} %bitcast.364, bf16[32,3,128,128]{3,2,1,0:T(8,128)(2,1)S(1)} %copy-done.2, f32[32,128]{1,0:T(8,128)S(1)} %multiply_add_fusion.1, bf16[32,64,128]{2,1,0:T(8,128)(2,1)} %param.17, f32[32,64,128]{2,1,0:T(8,128)} %get-tuple-element.32, ...), kind=kOutput, calls=%fused_computation.199 | convolution fusion | flops 203948032 | bytes 8929280 | tf_op jit(solution)/shard_map/nkrb,nkbc->nrc/dot_general | solution.py:59
  314.8 1.9 collective-permute-start.34
  316.7 7.2 %collective-permute-start.35 = (bf16[2,64,128]{2,1,0:T(8,128)(2,1)S(1)}, bf16[2,64,128]{2,1,0:T(8,128)(2,1)S(1)}, u32[]{:S(2)}, u32[]{:S(2)}) collective-permute-start(bf16[2,64,128]{2,1,0:T(8,128)(2,1)S(1)} %get-tuple-element.12), channel_id=1, source_target_pairs={{1,0},{2,1},{3,2},{4,3},{5,4},{6,5},{7,6},{8,7},{9,8},{10,9},{11,1... | collective-permute-start | bytes 98312 | tf_op jit(solution)/shard_map/ppermute | solution.py:26
  324.0 1.6 collective-permute-done.35
  326.4 3.0 gather_fusion.14
  329.5 3.6 %fusion.13 = f32[32,64,128]{2,1,0:T(8,128)} fusion(f32[32,64,128]{2,1,0:T(8,128)} %get-tuple-element.40, bf16[32,3,64,128]{3,2,1,0:T(8,128)(2,1)} %bitcast.365, bf16[32,3,128,128]{3,2,1,0:T(8,128)(2,1)S(1)} %copy-done.2, bf16[32,64,128]{2,1,0:T(8,128)(2,1)} %param.17, f32[32,128]{1,0:T(8,128)S(1)} %multiply_add_fusion.1), kind=kOutput, calls=%fused_computation.42 | convolution fusion | flops 203423744 | bytes 7356416 | tf_op jit(solution)/shard_map/nkrb,nkbc->nrc/dot_general | solution.py:59
  (159 shorter events, 30.8 us)
Async XLA Ops:
  0.0 192.7 %copy-start = (bf16[128,1024]{1,0:T(8,128)(2,1)S(1)}, bf16[128,1024]{1,0:T(8,128)(2,1)}, u32[]{:S(2)}) copy-start(bf16[128,1024]{1,0:T(8,128)(2,1)} %param.33) | copy-start | bytes 786436
  0.0 2.6 copy-start.10
  0.0 2.7 copy-start.7
  0.0 12.0 %copy-start.16 = (s32[32,3]{0,1:T(4,128)S(1)}, s32[32,3]{0,1:T(4,128)}, u32[]{:S(2)}) copy-start(s32[32,3]{0,1:T(4,128)} %param.19) | copy-start | bytes 1156
  0.0 12.2 %copy-start.5 = (bf16[8,3,128,128]{3,2,1,0:T(8,128)(2,1)S(1)}, bf16[8,3,128,128]{3,2,1,0:T(8,128)(2,1)}, u32[]{:S(2)}) copy-start(bf16[8,3,128,128]{3,2,1,0:T(8,128)(2,1)} %param.23) | copy-start | bytes 2359300
  2.6 9.8 %copy-start.11 = (s32[32,128]{1,0:T(8,128)S(1)}, s32[32,128]{1,0:T(8,128)}, u32[]{:S(2)}) copy-start(s32[32,128]{1,0:T(8,128)} %param.22) | copy-start | bytes 49156
  2.6 9.8 %copy-start.12 = (s32[32,128]{1,0:T(8,128)S(1)}, s32[32,128]{1,0:T(8,128)}, u32[]{:S(2)}) copy-start(s32[32,128]{1,0:T(8,128)} %param.21) | copy-start | bytes 49156
  2.6 9.8 %copy-start.13 = (f32[8,128]{1,0:T(8,128)S(1)}, f32[8,128]{1,0:T(8,128)}, u32[]{:S(2)}) copy-start(f32[8,128]{1,0:T(8,128)} %param.25) | copy-start | bytes 12292
  2.9 9.6 %collective-permute-start = (bf16[2,64,128]{2,1,0:T(8,128)(2,1)S(1)}, bf16[2,64,128]{2,1,0:T(8,128)(2,1)S(1)}, u32[]{:S(2)}, u32[]{:S(2)}) collective-permute-start(bf16[2,64,128]{2,1,0:T(8,128)(2,1)S(1)} %get-tuple-element.17), channel_id=1, source_target_pairs={{0,1},{1,2},{2,3},{3,4},{4,5},{5,6},{6,7},{7,8},{8,9},{9,10},{10,1... | collective-permute-start | bytes 98312 | tf_op jit(solution)/shard_map/ppermute | solution.py:23
  6.3 7.3 %collective-permute-start.1 = (bf16[2,64,128]{2,1,0:T(8,128)(2,1)S(1)}, bf16[2,64,128]{2,1,0:T(8,128)(2,1)S(1)}, u32[]{:S(2)}, u32[]{:S(2)}) collective-permute-start(bf16[2,64,128]{2,1,0:T(8,128)(2,1)S(1)} %get-tuple-element.18), channel_id=1, source_target_pairs={{1,0},{2,1},{3,2},{4,3},{5,4},{6,5},{7,6},{8,7},{9,8},{10,9},{11,1... | collective-permute-start | bytes 98312 | tf_op jit(solution)/shard_map/ppermute | solution.py:26
  14.5 3.2 copy-start.1
  17.7 13.9 %copy-start.14 = (s32[8,128]{1,0:T(8,128)S(1)}, s32[8,128]{1,0:T(8,128)}, u32[]{:S(2)}) copy-start(s32[8,128]{1,0:T(8,128)} %param.27) | copy-start | bytes 12292
  17.7 13.9 %copy-start.15 = (s32[8,128]{1,0:T(8,128)S(1)}, s32[8,128]{1,0:T(8,128)}, u32[]{:S(2)}) copy-start(s32[8,128]{1,0:T(8,128)} %param.26) | copy-start | bytes 12292
  21.0 0.8 copy-start.9
  22.4 9.2 %collective-permute-start.2 = (bf16[2,64,128]{2,1,0:T(8,128)(2,1)}, bf16[2,64,128]{2,1,0:T(8,128)(2,1)S(1)}, u32[]{:S(2)}, u32[]{:S(2)}) collective-permute-start(bf16[2,64,128]{2,1,0:T(8,128)(2,1)} %get-tuple-element.15), channel_id=1, source_target_pairs={{0,1},{1,2},{2,3},{3,4},{4,5},{5,6},{6,7},{7,8},{8,9},{9,10},{10,1... | collective-permute-start | bytes 98312 | tf_op jit(solution)/shard_map/ppermute | solution.py:23
  25.3 7.9 %collective-permute-start.3 = (bf16[2,64,128]{2,1,0:T(8,128)(2,1)S(1)}, bf16[2,64,128]{2,1,0:T(8,128)(2,1)S(1)}, u32[]{:S(2)}, u32[]{:S(2)}) collective-permute-start(bf16[2,64,128]{2,1,0:T(8,128)(2,1)S(1)} %get-tuple-element.16), channel_id=1, source_target_pairs={{1,0},{2,1},{3,2},{4,3},{5,4},{6,5},{7,6},{8,7},{9,8},{10,9},{11,1... | collective-permute-start | bytes 98312 | tf_op jit(solution)/shard_map/ppermute | solution.py:26
  68.0 9.3 %copy-start.17 = (s32[8,3]{0,1:T(4,128)S(1)}, s32[8,3]{0,1:T(4,128)}, u32[]{:S(2)}) copy-start(s32[8,3]{0,1:T(4,128)} %param.24) | copy-start | bytes 292
  68.0 9.5 %copy-start.8 = (bf16[2,3,128,128]{3,2,1,0:T(8,128)(2,1)S(1)}, bf16[2,3,128,128]{3,2,1,0:T(8,128)(2,1)}, u32[]{:S(2)}) copy-start(bf16[2,3,128,128]{3,2,1,0:T(8,128)(2,1)} %param.28) | copy-start | bytes 589828
  68.2 11.9 %collective-permute-start.4 = (bf16[1024,64]{1,0:T(8,128)(2,1)S(1)}, bf16[1024,64]{1,0:T(8,128)(2,1)S(1)}, u32[]{:S(2)}, u32[]{:S(2)}) collective-permute-start(bf16[1024,64]{1,0:T(8,128)(2,1)S(1)} %get-tuple-element.9), channel_id=1, source_target_pairs={{0,1},{1,2},{2,3},{3,4},{4,5},{5,6},{6,7},{7,8},{8,9},{9,10},{10,1... | collective-permute-start | bytes 393224 | tf_op jit(solution)/shard_map/ppermute | solution.py:38
  70.1 13.7 %collective-permute-start.5 = (bf16[1024,64]{1,0:T(8,128)(2,1)S(1)}, bf16[1024,64]{1,0:T(8,128)(2,1)}, u32[]{:S(2)}, u32[]{:S(2)}) collective-permute-start(bf16[1024,64]{1,0:T(8,128)(2,1)S(1)} %get-tuple-element.10), channel_id=1, source_target_pairs={{1,0},{2,1},{3,2},{4,3},{5,4},{6,5},{7,6},{8,7},{9,8},{10,9},{11,1... | collective-permute-start | bytes 393224 | tf_op jit(solution)/shard_map/ppermute | solution.py:38
  84.8 11.7 %copy-start.6 = (bf16[8,3,128,128]{3,2,1,0:T(8,128)(2,1)S(1)}, bf16[8,3,128,128]{3,2,1,0:T(8,128)(2,1)}, u32[]{:S(2)}) copy-start(bf16[8,3,128,128]{3,2,1,0:T(8,128)(2,1)} %param.23) | copy-start | bytes 2359300
  85.1 9.2 %collective-permute-start.6 = (bf16[2,64,128]{2,1,0:T(8,128)(2,1)S(1)}, bf16[2,64,128]{2,1,0:T(8,128)(2,1)S(1)}, u32[]{:S(2)}, u32[]{:S(2)}) collective-permute-start(bf16[2,64,128]{2,1,0:T(8,128)(2,1)S(1)} %get-tuple-element.27), channel_id=1, source_target_pairs={{0,1},{1,2},{2,3},{3,4},{4,5},{5,6},{6,7},{7,8},{8,9},{9,10},{10,1... | collective-permute-start | bytes 98312 | tf_op jit(solution)/shard_map/ppermute | solution.py:23
  87.0 8.8 %collective-permute-start.7 = (bf16[2,64,128]{2,1,0:T(8,128)(2,1)S(1)}, bf16[2,64,128]{2,1,0:T(8,128)(2,1)S(1)}, u32[]{:S(2)}, u32[]{:S(2)}) collective-permute-start(bf16[2,64,128]{2,1,0:T(8,128)(2,1)S(1)} %get-tuple-element.28), channel_id=1, source_target_pairs={{1,0},{2,1},{3,2},{4,3},{5,4},{6,5},{7,6},{8,7},{9,8},{10,9},{11,1... | collective-permute-start | bytes 98312 | tf_op jit(solution)/shard_map/ppermute | solution.py:26
  96.5 9.5 %copy-start.18 = (f32[2,128]{1,0:T(2,128)S(1)}, f32[2,128]{1,0:T(2,128)}, u32[]{:S(2)}) copy-start(f32[2,128]{1,0:T(2,128)} %param.30) | copy-start | bytes 3076
  96.8 9.2 %collective-permute-start.8 = (bf16[2,64,128]{2,1,0:T(8,128)(2,1)S(1)}, bf16[2,64,128]{2,1,0:T(8,128)(2,1)S(1)}, u32[]{:S(2)}, u32[]{:S(2)}) collective-permute-start(bf16[2,64,128]{2,1,0:T(8,128)(2,1)S(1)} %get-tuple-element.25), channel_id=1, source_target_pairs={{0,1},{1,2},{2,3},{3,4},{4,5},{5,6},{6,7},{7,8},{8,9},{9,10},{10,1... | collective-permute-start | bytes 98312 | tf_op jit(solution)/shard_map/ppermute | solution.py:23
  98.8 8.8 %collective-permute-start.9 = (bf16[2,64,128]{2,1,0:T(8,128)(2,1)S(1)}, bf16[2,64,128]{2,1,0:T(8,128)(2,1)S(1)}, u32[]{:S(2)}, u32[]{:S(2)}) collective-permute-start(bf16[2,64,128]{2,1,0:T(8,128)(2,1)S(1)} %get-tuple-element.26), channel_id=1, source_target_pairs={{1,0},{2,1},{3,2},{4,3},{5,4},{6,5},{7,6},{8,7},{9,8},{10,9},{11,1... | collective-permute-start | bytes 98312 | tf_op jit(solution)/shard_map/ppermute | solution.py:26
  108.5 15.6 %copy-start.21 = (s32[2,3]{1,0:T(2,128)S(1)}, s32[2,3]{1,0:T(2,128)}, u32[]{:S(2)}) copy-start(s32[2,3]{1,0:T(2,128)} %param.29) | copy-start | bytes 76
  108.8 38.2 %copy-start.19 = (s32[2,128]{1,0:T(2,128)S(1)}, s32[2,128]{1,0:T(2,128)}, u32[]{:S(2)}) copy-start(s32[2,128]{1,0:T(2,128)} %param.32) | copy-start | bytes 3076
  108.8 38.2 %copy-start.20 = (s32[2,128]{1,0:T(2,128)S(1)}, s32[2,128]{1,0:T(2,128)}, u32[]{:S(2)}) copy-start(s32[2,128]{1,0:T(2,128)} %param.31) | copy-start | bytes 3076
  115.0 9.3 %collective-permute-start.10 = (bf16[256,64]{1,0:T(8,128)(2,1)S(1)}, bf16[256,64]{1,0:T(8,128)(2,1)S(1)}, u32[]{:S(2)}, u32[]{:S(2)}) collective-permute-start(bf16[256,64]{1,0:T(8,128)(2,1)S(1)} %get-tuple-element.19), channel_id=1, source_target_pairs={{0,1},{1,2},{2,3},{3,4},{4,5},{5,6},{6,7},{7,8},{8,9},{9,10},{10,1... | collective-permute-start | bytes 98312 | tf_op jit(solution)/shard_map/ppermute | solution.py:38
  116.9 9.1 %collective-permute-start.11 = (bf16[256,64]{1,0:T(8,128)(2,1)S(1)}, bf16[256,64]{1,0:T(8,128)(2,1)S(1)}, u32[]{:S(2)}, u32[]{:S(2)}) collective-permute-start(bf16[256,64]{1,0:T(8,128)(2,1)S(1)} %get-tuple-element.20), channel_id=1, source_target_pairs={{1,0},{2,1},{3,2},{4,3},{5,4},{6,5},{7,6},{8,7},{9,8},{10,9},{11,1... | collective-permute-start | bytes 98312 | tf_op jit(solution)/shard_map/ppermute | solution.py:38
  126.2 9.2 %collective-permute-start.12 = (bf16[2,64,128]{2,1,0:T(8,128)(2,1)S(1)}, bf16[2,64,128]{2,1,0:T(8,128)(2,1)S(1)}, u32[]{:S(2)}, u32[]{:S(2)}) collective-permute-start(bf16[2,64,128]{2,1,0:T(8,128)(2,1)S(1)} %fusion.94), channel_id=1, source_target_pairs={{0,1},{1,2},{2,3},{3,4},{4,5},{5,6},{6,7},{7,8},{8,9},{9,10},{10,1... | collective-permute-start | bytes 98312 | tf_op jit(solution)/shard_map/ppermute | solution.py:23
  128.1 8.9 %collective-permute-start.13 = (bf16[2,64,128]{2,1,0:T(8,128)(2,1)S(1)}, bf16[2,64,128]{2,1,0:T(8,128)(2,1)S(1)}, u32[]{:S(2)}, u32[]{:S(2)}) collective-permute-start(bf16[2,64,128]{2,1,0:T(8,128)(2,1)S(1)} %fusion.94), channel_id=1, source_target_pairs={{1,0},{2,1},{3,2},{4,3},{5,4},{6,5},{7,6},{8,7},{9,8},{10,9},{11,1... | collective-permute-start | bytes 98312 | tf_op jit(solution)/shard_map/ppermute | solution.py:26
  137.7 9.2 %collective-permute-start.14 = (bf16[2,64,128]{2,1,0:T(8,128)(2,1)S(1)}, bf16[2,64,128]{2,1,0:T(8,128)(2,1)S(1)}, u32[]{:S(2)}, u32[]{:S(2)}) collective-permute-start(bf16[2,64,128]{2,1,0:T(8,128)(2,1)S(1)} %get-tuple-element.5), channel_id=1, source_target_pairs={{0,1},{1,2},{2,3},{3,4},{4,5},{5,6},{6,7},{7,8},{8,9},{9,10},{10,1... | collective-permute-start | bytes 98312 | tf_op jit(solution)/shard_map/ppermute | solution.py:23
  139.7 8.8 %collective-permute-start.15 = (bf16[2,64,128]{2,1,0:T(8,128)(2,1)S(1)}, bf16[2,64,128]{2,1,0:T(8,128)(2,1)S(1)}, u32[]{:S(2)}, u32[]{:S(2)}) collective-permute-start(bf16[2,64,128]{2,1,0:T(8,128)(2,1)S(1)} %get-tuple-element.5), channel_id=1, source_target_pairs={{1,0},{2,1},{3,2},{4,3},{5,4},{6,5},{7,6},{8,7},{9,8},{10,9},{11,1... | collective-permute-start | bytes 98312 | tf_op jit(solution)/shard_map/ppermute | solution.py:26
  151.1 9.3 %collective-permute-start.16 = (bf16[128,64]{1,0:T(8,128)(2,1)S(1)}, bf16[128,64]{1,0:T(8,128)(2,1)S(1)}, u32[]{:S(2)}, u32[]{:S(2)}) collective-permute-start(bf16[128,64]{1,0:T(8,128)(2,1)S(1)} %get-tuple-element.29), channel_id=1, source_target_pairs={{0,1},{1,2},{2,3},{3,4},{4,5},{5,6},{6,7},{7,8},{8,9},{9,10},{10,1... | collective-permute-start | bytes 49160 | tf_op jit(solution)/shard_map/ppermute | solution.py:38
  153.0 8.9 %collective-permute-start.17 = (bf16[128,64]{1,0:T(8,128)(2,1)S(1)}, bf16[128,64]{1,0:T(8,128)(2,1)S(1)}, u32[]{:S(2)}, u32[]{:S(2)}) collective-permute-start(bf16[128,64]{1,0:T(8,128)(2,1)S(1)} %get-tuple-element.30), channel_id=1, source_target_pairs={{1,0},{2,1},{3,2},{4,3},{5,4},{6,5},{7,6},{8,7},{9,8},{10,9},{11,1... | collective-permute-start | bytes 49160 | tf_op jit(solution)/shard_map/ppermute | solution.py:38
  193.0 9.2 %collective-permute-start.18 = (bf16[128,64]{0,1:T(8,128)(2,1)S(1)}, bf16[128,64]{0,1:T(8,128)(2,1)S(1)}, u32[]{:S(2)}, u32[]{:S(2)}) collective-permute-start(bf16[128,64]{0,1:T(8,128)(2,1)S(1)} %fusion.46), channel_id=1, source_target_pairs={{0,1},{1,2},{2,3},{3,4},{4,5},{5,6},{6,7},{7,8},{8,9},{9,10},{10,1... | collective-permute-start | bytes 49160 | tf_op jit(solution)/shard_map/ppermute | solution.py:23
  194.9 8.7 %collective-permute-start.19 = (bf16[128,64]{0,1:T(8,128)(2,1)S(1)}, bf16[128,64]{0,1:T(8,128)(2,1)S(1)}, u32[]{:S(2)}, u32[]{:S(2)}) collective-permute-start(bf16[128,64]{0,1:T(8,128)(2,1)S(1)} %fusion.46), channel_id=1, source_target_pairs={{1,0},{2,1},{3,2},{4,3},{5,4},{6,5},{7,6},{8,7},{9,8},{10,9},{11,1... | collective-permute-start | bytes 49160 | tf_op jit(solution)/shard_map/ppermute | solution.py:26
  204.5 9.2 %collective-permute-start.20 = (bf16[2,64,128]{2,1,0:T(8,128)(2,1)S(1)}, bf16[2,64,128]{2,1,0:T(8,128)(2,1)S(1)}, u32[]{:S(2)}, u32[]{:S(2)}) collective-permute-start(bf16[2,64,128]{2,1,0:T(8,128)(2,1)S(1)} %fusion.96), channel_id=1, source_target_pairs={{0,1},{1,2},{2,3},{3,4},{4,5},{5,6},{6,7},{7,8},{8,9},{9,10},{10,1... | collective-permute-start | bytes 98312 | tf_op jit(solution)/shard_map/ppermute | solution.py:23
  206.5 8.8 %collective-permute-start.21 = (bf16[2,64,128]{2,1,0:T(8,128)(2,1)S(1)}, bf16[2,64,128]{2,1,0:T(8,128)(2,1)S(1)}, u32[]{:S(2)}, u32[]{:S(2)}) collective-permute-start(bf16[2,64,128]{2,1,0:T(8,128)(2,1)S(1)} %fusion.96), channel_id=1, source_target_pairs={{1,0},{2,1},{3,2},{4,3},{5,4},{6,5},{7,6},{8,7},{9,8},{10,9},{11,1... | collective-permute-start | bytes 98312 | tf_op jit(solution)/shard_map/ppermute | solution.py:26
  216.1 9.2 %collective-permute-start.22 = (bf16[2,64,128]{2,1,0:T(8,128)(2,1)S(1)}, bf16[2,64,128]{2,1,0:T(8,128)(2,1)S(1)}, u32[]{:S(2)}, u32[]{:S(2)}) collective-permute-start(bf16[2,64,128]{2,1,0:T(8,128)(2,1)S(1)} %get-tuple-element.35), channel_id=1, source_target_pairs={{0,1},{1,2},{2,3},{3,4},{4,5},{5,6},{6,7},{7,8},{8,9},{9,10},{10,1... | collective-permute-start | bytes 98312 | tf_op jit(solution)/shard_map/ppermute | solution.py:23
  218.0 8.8 %collective-permute-start.23 = (bf16[2,64,128]{2,1,0:T(8,128)(2,1)S(1)}, bf16[2,64,128]{2,1,0:T(8,128)(2,1)S(1)}, u32[]{:S(2)}, u32[]{:S(2)}) collective-permute-start(bf16[2,64,128]{2,1,0:T(8,128)(2,1)S(1)} %get-tuple-element.35), channel_id=1, source_target_pairs={{1,0},{2,1},{3,2},{4,3},{5,4},{6,5},{7,6},{8,7},{9,8},{10,9},{11,1... | collective-permute-start | bytes 98312 | tf_op jit(solution)/shard_map/ppermute | solution.py:26
  227.7 9.2 %collective-permute-start.24 = (bf16[256,64]{1,0:T(8,128)(2,1)S(1)}, bf16[256,64]{1,0:T(8,128)(2,1)S(1)}, u32[]{:S(2)}, u32[]{:S(2)}) collective-permute-start(bf16[256,64]{1,0:T(8,128)(2,1)S(1)} %bitcast.378), channel_id=1, source_target_pairs={{0,1},{1,2},{2,3},{3,4},{4,5},{5,6},{6,7},{7,8},{8,9},{9,10},{10,1... | collective-permute-start | bytes 98312 | tf_op jit(solution)/shard_map/ppermute | solution.py:23
  229.7 9.1 %collective-permute-start.25 = (bf16[256,64]{1,0:T(8,128)(2,1)S(1)}, bf16[256,64]{1,0:T(8,128)(2,1)S(1)}, u32[]{:S(2)}, u32[]{:S(2)}) collective-permute-start(bf16[256,64]{1,0:T(8,128)(2,1)S(1)} %bitcast.379), channel_id=1, source_target_pairs={{1,0},{2,1},{3,2},{4,3},{5,4},{6,5},{7,6},{8,7},{9,8},{10,9},{11,1... | collective-permute-start | bytes 98312 | tf_op jit(solution)/shard_map/ppermute | solution.py:26
  241.9 9.2 %collective-permute-start.26 = (bf16[2,64,128]{2,1,0:T(8,128)(2,1)S(1)}, bf16[2,64,128]{2,1,0:T(8,128)(2,1)S(1)}, u32[]{:S(2)}, u32[]{:S(2)}) collective-permute-start(bf16[2,64,128]{2,1,0:T(8,128)(2,1)S(1)} %get-tuple-element.23), channel_id=1, source_target_pairs={{0,1},{1,2},{2,3},{3,4},{4,5},{5,6},{6,7},{7,8},{8,9},{9,10},{10,1... | collective-permute-start | bytes 98312 | tf_op jit(solution)/shard_map/ppermute | solution.py:23
  243.8 8.9 %collective-permute-start.27 = (bf16[2,64,128]{2,1,0:T(8,128)(2,1)S(1)}, bf16[2,64,128]{2,1,0:T(8,128)(2,1)S(1)}, u32[]{:S(2)}, u32[]{:S(2)}) collective-permute-start(bf16[2,64,128]{2,1,0:T(8,128)(2,1)S(1)} %get-tuple-element.24), channel_id=1, source_target_pairs={{1,0},{2,1},{3,2},{4,3},{5,4},{6,5},{7,6},{8,7},{9,8},{10,9},{11,1... | collective-permute-start | bytes 98312 | tf_op jit(solution)/shard_map/ppermute | solution.py:26
  253.7 9.2 %collective-permute-start.28 = (bf16[2,64,128]{2,1,0:T(8,128)(2,1)S(1)}, bf16[2,64,128]{2,1,0:T(8,128)(2,1)S(1)}, u32[]{:S(2)}, u32[]{:S(2)}) collective-permute-start(bf16[2,64,128]{2,1,0:T(8,128)(2,1)S(1)} %get-tuple-element.21), channel_id=1, source_target_pairs={{0,1},{1,2},{2,3},{3,4},{4,5},{5,6},{6,7},{7,8},{8,9},{9,10},{10,1... | collective-permute-start | bytes 98312 | tf_op jit(solution)/shard_map/ppermute | solution.py:23
  255.6 8.8 %collective-permute-start.29 = (bf16[2,64,128]{2,1,0:T(8,128)(2,1)S(1)}, bf16[2,64,128]{2,1,0:T(8,128)(2,1)S(1)}, u32[]{:S(2)}, u32[]{:S(2)}) collective-permute-start(bf16[2,64,128]{2,1,0:T(8,128)(2,1)S(1)} %get-tuple-element.22), channel_id=1, source_target_pairs={{1,0},{2,1},{3,2},{4,3},{5,4},{6,5},{7,6},{8,7},{9,8},{10,9},{11,1... | collective-permute-start | bytes 98312 | tf_op jit(solution)/shard_map/ppermute | solution.py:26
  265.7 11.7 %collective-permute-start.30 = (bf16[1024,64]{1,0:T(8,128)(2,1)S(1)}, bf16[1024,64]{1,0:T(8,128)(2,1)S(1)}, u32[]{:S(2)}, u32[]{:S(2)}) collective-permute-start(bf16[1024,64]{1,0:T(8,128)(2,1)S(1)} %bitcast.368), channel_id=1, source_target_pairs={{0,1},{1,2},{2,3},{3,4},{4,5},{5,6},{6,7},{7,8},{8,9},{9,10},{10,1... | collective-permute-start | bytes 393224 | tf_op jit(solution)/shard_map/ppermute | solution.py:23
  267.6 11.5 %collective-permute-start.31 = (bf16[1024,64]{1,0:T(8,128)(2,1)S(1)}, bf16[1024,64]{1,0:T(8,128)(2,1)S(1)}, u32[]{:S(2)}, u32[]{:S(2)}) collective-permute-start(bf16[1024,64]{1,0:T(8,128)(2,1)S(1)} %bitcast.369), channel_id=1, source_target_pairs={{1,0},{2,1},{3,2},{4,3},{5,4},{6,5},{7,6},{8,7},{9,8},{10,9},{11,1... | collective-permute-start | bytes 393224 | tf_op jit(solution)/shard_map/ppermute | solution.py:26
  293.3 2.3 copy-start.3
  295.6 11.1 %copy-start.4 = (f32[32,128,64]{1,2,0:T(8,128)}, f32[32,128,64]{1,2,0:T(8,128)S(1)}, u32[]{:S(2)}) copy-start(f32[32,128,64]{1,2,0:T(8,128)S(1)} %copy.93) | copy-start | bytes 3145732
  295.8 9.3 %collective-permute-start.32 = (bf16[2,64,128]{2,1,0:T(8,128)(2,1)S(1)}, bf16[2,64,128]{2,1,0:T(8,128)(2,1)S(1)}, u32[]{:S(2)}, u32[]{:S(2)}) collective-permute-start(bf16[2,64,128]{2,1,0:T(8,128)(2,1)S(1)} %get-tuple-element.13), channel_id=1, source_target_pairs={{0,1},{1,2},{2,3},{3,4},{4,5},{5,6},{6,7},{7,8},{8,9},{9,10},{10,1... | collective-permute-start | bytes 98312 | tf_op jit(solution)/shard_map/ppermute | solution.py:23
  297.7 9.0 %collective-permute-start.33 = (bf16[2,64,128]{2,1,0:T(8,128)(2,1)S(1)}, bf16[2,64,128]{2,1,0:T(8,128)(2,1)S(1)}, u32[]{:S(2)}, u32[]{:S(2)}) collective-permute-start(bf16[2,64,128]{2,1,0:T(8,128)(2,1)S(1)} %get-tuple-element.14), channel_id=1, source_target_pairs={{1,0},{2,1},{3,2},{4,3},{5,4},{6,5},{7,6},{8,7},{9,8},{10,9},{11,1... | collective-permute-start | bytes 98312 | tf_op jit(solution)/shard_map/ppermute | solution.py:26
  307.6 3.2 copy-start.2
  314.8 9.2 %collective-permute-start.34 = (bf16[2,64,128]{2,1,0:T(8,128)(2,1)S(1)}, bf16[2,64,128]{2,1,0:T(8,128)(2,1)S(1)}, u32[]{:S(2)}, u32[]{:S(2)}) collective-permute-start(bf16[2,64,128]{2,1,0:T(8,128)(2,1)S(1)} %get-tuple-element.11), channel_id=1, source_target_pairs={{0,1},{1,2},{2,3},{3,4},{4,5},{5,6},{6,7},{7,8},{8,9},{9,10},{10,1... | collective-permute-start | bytes 98312 | tf_op jit(solution)/shard_map/ppermute | solution.py:23
  316.7 8.8 %collective-permute-start.35 = (bf16[2,64,128]{2,1,0:T(8,128)(2,1)S(1)}, bf16[2,64,128]{2,1,0:T(8,128)(2,1)S(1)}, u32[]{:S(2)}, u32[]{:S(2)}) collective-permute-start(bf16[2,64,128]{2,1,0:T(8,128)(2,1)S(1)} %get-tuple-element.12), channel_id=1, source_target_pairs={{1,0},{2,1},{3,2},{4,3},{5,4},{6,5},{7,6},{8,7},{9,8},{10,9},{11,1... | collective-permute-start | bytes 98312 | tf_op jit(solution)/shard_map/ppermute | solution.py:26
where the time goes:
time: 336 us; the launch traced here: 333 us
  starting transfers between devices  166 us (49%)
  local copies, waits for them, and re-layouts  43.6 us (13%)
  other arithmetic  40.2 us (12%)
  waiting for transfers between devices  34.9 us (10%)
  blocking collectives  30.8 us (9%)
  matrix products  16.8 us (5%)
    ppermute x15, starting transfers between devices, extended_2(): lax.ppermute(lax.slice_in_dim(block, 0, width, axis=dim), axis, backward)  107 us
    ppermute x15, starting transfers between devices, extended_2(): lax.ppermute(lax.slice_in_dim(block, block.shape[dim] - width, None, axis...  31.2 us
    scatter-add x3, other arithmetic, restrict(): jax.ops.segment_sum(gather_rows(residual), targets, num_segments=3 * coar...  30.8 us
    all_gather x1, blocking collectives, coarse_solve(): lax.all_gather(rounded, 'col', axis=1, tiled=True)  30.8 us
    ppermute x6, starting transfers between devices, passed_along(): lax.ppermute(value, axis, [(source, source + steps) for source in range(i...  27.6 us
    ppermute x15, waiting for transfers between devices, extended_2(): lax.ppermute(lax.slice_in_dim(block, 0, width, axis=dim), axis, backward)  23.1 us
    gather x3, local copies, waits for them, and re-layouts, prolong(): return current_iterate + make_blocks(extended[targets])  17.7 us
    gather x12, local copies, waits for them, and re-layouts, apply_operator(): picked = extended[columns - offset]  17.2 us
  transfers between devices with their start and end apart: 36, of which 20 were waited for; matrix products, arithmetic and copies ran while one was open for 0% of the time, Pallas kernels for 0%

commit v1 on v0

v1 whole, which is shorter than its diff:
```python
import functools

import jax
import jax.numpy as jnp
from jax import lax
from jax.experimental import pallas as pl
from jax.experimental.pallas import tpu as pltpu
from jax.sharding import PartitionSpec as P

F32 = jnp.float32
BF16 = jnp.bfloat16
MESH = pl.DeviceIdType.MESH
DAMPING = 0.8
SPLIT_OWN = False


def loop(low, high, body, unroll=4):
    count = high - low
    if count <= 0:
        return
    while count % unroll:
        unroll -= 1

    if count == unroll:
        for inner in range(count):
            body(low + inner)
        return

    def step(outer, carry):
        for inner in range(unroll):
            body(low + outer * unroll + inner)
        return carry

    lax.fori_loop(0, count // unroll, step, 0)


class Level:
    def __init__(self, blocks, coarse, rhs_count, bs, k, ref, hbm, columns, ops):
        self.n, self.t, self.r, self.bs, self.k = blocks, coarse, rhs_count, bs, k
        self.ref, self.hbm, self.columns, self.ops = ref, hbm, columns, ops
        self.single = blocks < 4
        self.base = ops.me * blocks
        self.scale = 1.0 / (k * bs)

    def edges(self):
        n = self.n
        if self.single:
            return list(range(n))
        return [0, 1, n - 2, n - 1]

    def inner(self):
        return (0, 0) if self.single else (2, self.n - 2)

    def make_diagonal(self, b):
        w = self.ref["w"][b]
        total = jnp.dot(jnp.ones((8, w.shape[0]), BF16), w, preferred_element_type=F32)
        degree = self.ref["deg"][pl.ds(b, 1), :]
        g = degree + total * self.scale
        self.ref["g"][b] = g
        self.ref["gi"][b] = DAMPING / g

    def row(self, name, b):
        value = self.ref[name][b, 0:1, :]
        return jnp.broadcast_to(value, (self.r, self.bs))

    def f(self, b):
        return self.ref["f"][b].astype(F32)

    def product(self, i, b, where):
        if where == "inner":
            buf, offset = self.ref["vb"].at[i], self.base
        elif where == "low":
            buf, offset = self.ref[f"lo{i}"], self.base - 2
        else:
            buf, offset = self.ref[f"hi{i}"], self.base + self.n - 4
        top = buf.shape[0] - 1
        picked = [
            buf[jnp.clip(self.columns[b, k] - offset, 0, top)] for k in range(self.k)
        ]
        left = jnp.concatenate(picked, axis=1)
        return jnp.dot(left, self.ref["w"][b], preferred_element_type=F32) * self.scale

    def halo_copies(self, i):
        n, ops, vb = self.n, self.ops, self.ref["vb"].at[i]
        if self.single:
            low_dst, high_dst = self.ref[f"lo{i}"].at[0:2], self.ref[f"lo{i}"].at[4:6]
        else:
            low_dst, high_dst = self.ref[f"lo{i}"].at[0:2], self.ref[f"hi{i}"].at[4:6]
        return ops.pair(vb.at[n - 2 : n], low_dst, vb.at[0:2], high_dst, self.ref["sem"] + i)

    def fill_edges(self, i):
        n = self.n
        if self.single:
            self.ref[f"lo{i}"][2:4] = self.ref["vb"][i, 0:2]
        else:
            self.ref[f"lo{i}"][2:6] = self.ref["vb"][i, 0:4]
            self.ref[f"hi{i}"][0:4] = self.ref["vb"][i, n - 4 : n]

    def run_edges(self, body):
        for b in self.edges():
            body(b, "low" if b < 2 else "high")

    def apply(self, i, body):
        loop(*self.inner(), lambda b: body(b, "inner"))
        self.fill_edges(i)
        self.ops.wait(self.halo_copies(i))
        self.run_edges(body)

    def start_block(self, b):
        self.ref["vb"][0, b] = (self.row("gi", b) * self.f(b)).astype(BF16)

    def first_sweep(self, b, where):
        f, gi = self.f(b), self.row("gi", b)
        x0 = gi * f
        x = (1.0 - DAMPING) * x0 + gi * (f + self.product(0, b, where))
        self.ref["x"][b] = x
        self.ref["vb"][1, b] = x.astype(BF16)

    def residual(self, b, where):
        res = self.f(b) - self.row("g", b) * self.ref["x"][b] + self.product(1, b, where)
        rel = self.owner(b)
        columns = pl.ds(pl.multiple_of(b * self.bs, self.bs), self.bs)
        rows = self.r
        high = res.astype(BF16)
        zero = jnp.zeros_like(res)
        out = self.ref["res"]
        out[0:rows, columns] = jnp.where(rel < 0, res, zero).astype(BF16)
        out[rows : 2 * rows, columns] = jnp.where(rel > 0, res, zero).astype(BF16)
        own = jnp.where(rel == 0, res, zero)
        high = own.astype(BF16)
        out[2 * rows : 3 * rows, columns] = high
        if SPLIT_OWN:
            out[3 * rows : 4 * rows, columns] = (own - high.astype(F32)).astype(BF16)

    def owner(self, b):
        value = self.ref["own"][pl.ds(b, 1), :] - self.ops.me
        return jnp.broadcast_to(value, (self.r, self.bs))

    def make_onehot(self, b):
        columns = pl.ds(pl.multiple_of(b * self.bs, self.bs), self.bs)
        slots = jnp.broadcast_to(self.ref["slot"][pl.ds(b, 1), :], (self.t, self.bs))
        index = lax.broadcasted_iota(jnp.int32, (self.t, self.bs), 0)
        self.ref["oh"][:, columns] = jnp.where(index == slots, 1.0, 0.0).astype(BF16)

    def restricted(self, rows, put):
        tile = min(self.t, 256)

        def body(j):
            at = pl.ds(pl.multiple_of(j * tile, tile), tile)
            put(
                at,
                lax.dot_general(
                    self.ref["res"][rows, :],
                    self.ref["oh"][at, :],
                    (((1,), (1,)), ((), ())),
                    preferred_element_type=F32,
                ),
            )

        loop(0, self.t // tile, body, 1)

    def restrict_copies(self):
        out, got = self.ref["rout"], self.ref["rin"]
        return self.ops.pair(out.at[1], got.at[0], out.at[0], got.at[1], self.ref["sem"] + 4)

    def restrict(self, into):
        r = self.r

        def put_out(at, value):
            self.ref["rout"][0, :, at] = value[0:r].astype(BF16)
            self.ref["rout"][1, :, at] = value[r : 2 * r].astype(BF16)

        self.restricted(slice(0, 2 * r), put_out)
        copies = self.restrict_copies()
        self.ops.start(copies)

        def put_own(at, value):
            if SPLIT_OWN:
                value = value[0:r] + value[r : 2 * r]
            self.ref["rown"][:, at] = value

        self.restricted(slice(2 * r, (4 if SPLIT_OWN else 3) * r), put_own)
        self.ops.wait(copies)
        for block in range(self.t // self.bs):
            at = slice(block * self.bs, (block + 1) * self.bs)
            into(
                block,
                self.ref["rown"][:, at]
                + self.ref["rin"][0, :, at].astype(F32)
                + self.ref["rin"][1, :, at].astype(F32),
            )

    def down(self, into, while_first=None, while_second=None):
        self.ops.start(self.halo_copies(0))
        loop(*self.inner(), self.start_block)
        if while_first is not None:
            while_first()
        self.apply(0, self.first_sweep)
        self.ops.start(self.halo_copies(1))
        if while_second is not None:
            while_second()
        self.apply(1, self.residual)
        self.restrict(into)

    def prolong_copies(self):
        out, got = self.ref["uout"], self.ref["uin"]
        return self.ops.pair(out, got.at[0], out, got.at[1], self.ref["sem"] + 5)

    def pair_columns(self, pair):
        return pl.ds(pl.multiple_of(pair * 2 * self.bs, 2 * self.bs), 2 * self.bs)

    def add_own(self, pair):
        value = jnp.dot(
            self.ref["uout"][...], self.ref["oh"][:, self.pair_columns(pair)],
            preferred_element_type=F32,
        )
        for half in range(2):
            b = 2 * pair + half
            part = value[:, half * self.bs : (half + 1) * self.bs]
            self.ref["x"][b] = self.ref["x"][b] + jnp.where(self.owner(b) == 0, part, 0.0)

    def add_others(self, pair):
        left = jnp.concatenate([self.ref["uin"][0], self.ref["uin"][1]], axis=0)
        value = jnp.dot(
            left, self.ref["oh"][:, self.pair_columns(pair)], preferred_element_type=F32
        )
        for half in range(2):
            b = 2 * pair + half
            at = slice(half * self.bs, (half + 1) * self.bs)
            rel = self.owner(b)
            x = self.ref["x"][b]
            x = x + jnp.where(rel < 0, value[0 : self.r, at], 0.0)
            x = x + jnp.where(rel > 0, value[self.r : 2 * self.r, at], 0.0)
            self.ref["x"][b] = x
            self.ref["vb"][2, b] = x.astype(BF16)

    def sweep(self, i, last, out=None):
        def body(b, where):
            gi = self.row("gi", b)
            x = (1.0 - DAMPING) * self.ref["x"][b] + gi * (self.f(b) + self.product(i, b, where))
            self.ref["x"][b] = x
            if not last:
                self.ref["vb"][i + 1, b] = x.astype(BF16)
            elif out is not None:
                out(b, x)

        return body

    def up(self, out=None):
        copies = self.prolong_copies()
        self.ops.start(copies)
        pairs = self.n // 2
        loop(0, pairs, self.add_own, 2)
        self.ops.wait(copies)
        self.add_others(0)
        if not self.single:
            self.add_others(pairs - 1)
        self.ops.start(self.halo_copies(2))
        if not self.single:
            loop(1, pairs - 1, self.add_others, 2)
        self.apply(2, self.sweep(2, False))
        self.ops.start(self.halo_copies(3))
        self.apply(3, self.sweep(3, True, out))

    def drain(self):
        for i in range(4):
            self.ops.drain(self.halo_copies(i))
        self.ops.drain(self.restrict_copies())
        self.ops.drain(self.prolong_copies())

    def clear_ends(self):
        for name, first, last in (("rin", 0, 1), ("uin", 0, 1)):
            ref = self.ref[name]

            @pl.when(self.ops.me == 0)
            def _():
                ref[first] = jnp.zeros(ref.shape[1:], ref.dtype)

            @pl.when(self.ops.me == self.ops.total - 1)
            def _():
                ref[last] = jnp.zeros(ref.shape[1:], ref.dtype)


class Ops:
    def __init__(self, send, recv):
        self.send, self.recv = send, recv
        self.rows, self.cols = lax.axis_size("row"), lax.axis_size("col")
        self.total = self.rows * self.cols
        self.row, self.col = lax.axis_index("row"), lax.axis_index("col")
        self.me = self.row * self.cols + self.col
        right = jnp.minimum(self.me + 1, self.total - 1)
        left = jnp.maximum(self.me - 1, 0)
        self.right = (right // self.cols, right % self.cols)
        self.left = (left // self.cols, left % self.cols)
        self.has_right = self.me < self.total - 1
        self.has_left = self.me > 0

    def pair(self, to_right, at_right, to_left, at_left, slot):
        first = pltpu.make_async_remote_copy(
            to_right, at_right, self.send.at[slot, 0], self.recv.at[slot, 0],
            device_id=self.right, device_id_type=MESH,
        )
        second = pltpu.make_async_remote_copy(
            to_left, at_left, self.send.at[slot, 1], self.recv.at[slot, 1],
            device_id=self.left, device_id_type=MESH,
        )
        return first, second

    def start(self, copies):
        pl.when(self.has_right)(lambda: copies[0].start())
        pl.when(self.has_left)(lambda: copies[1].start())

    def wait(self, copies):
        pl.when(self.has_left)(lambda: copies[0].wait_recv())
        pl.when(self.has_right)(lambda: copies[1].wait_recv())

    def drain(self, copies):
        pl.when(self.has_right)(lambda: copies[0].wait_send())
        pl.when(self.has_left)(lambda: copies[1].wait_send())


LEVEL_HBM = ("w", "deg", "own", "slot")
LEVEL_SCRATCH = (
    "w", "deg", "own", "slot", "g", "gi", "x", "vb",
    "lo0", "lo1", "lo2", "lo3", "hi0", "hi1", "hi2", "hi3", "res", "oh",
    "rout", "rin", "rown", "uout", "uin",
)


def kernel(sizes, rhs_count, bs, k, coarse_all, *refs):
    refs = list(refs)
    take = lambda count: [refs.pop(0) for _ in range(count)]
    rhs_hbm, inverse_hbm = take(2)
    columns, hbm = [], []
    for _ in sizes:
        columns.append(refs.pop(0))
        hbm.append(dict(zip(LEVEL_HBM, take(4))))
    (out_hbm,) = take(1)
    scratch = [dict(zip(LEVEL_SCRATCH, take(len(LEVEL_SCRATCH)))) for _ in sizes]
    rhs, f_second, f_third, inverse, gathered, out = take(6)
    send, recv, gather_send, gather_recv, local, out_sem = take(6)

    ops = Ops(send, recv)
    levels = []
    for position, (n, t) in enumerate(sizes):
        ref = scratch[position]
        ref["sem"] = position * 6
        ref["f"] = (rhs, f_second, f_third)[position]
        levels.append(Level(n, t, rhs_count, bs, k, ref, hbm[position], columns[position], ops))
    fine, second, third = levels

    loads = []

    def load(src, dst):
        copy = pltpu.make_async_copy(src, dst, local.at[len(loads)])
        loads.append(copy)
        copy.start()
        return copy

    n = fine.n
    early = []
    for at in (slice(0, 2), slice(n - 2, n)):
        early.append(load(hbm[0]["w"].at[at], scratch[0]["w"].at[at]))
    early.append(load(hbm[0]["deg"], scratch[0]["deg"]))
    early.append(load(rhs_hbm, rhs))
    middle = load(hbm[0]["w"].at[2 : n - 2], scratch[0]["w"].at[2 : n - 2])
    later = [
        load(hbm[0][name], scratch[0][name]) for name in ("own", "slot")
    ]
    for position in (1, 2):
        later += [load(hbm[position][name], scratch[position][name]) for name in LEVEL_HBM]
    later.append(load(inverse_hbm, inverse))

    barrier = pltpu.get_barrier_semaphore()
    next_row = jnp.logical_and(ops.has_right, ops.col == ops.cols - 1)
    previous_row = jnp.logical_and(ops.has_left, ops.col == 0)
    pl.when(next_row)(
        lambda: pl.semaphore_signal(barrier, inc=1, device_id=ops.right, device_id_type=MESH)
    )
    pl.when(previous_row)(
        lambda: pl.semaphore_signal(barrier, inc=1, device_id=ops.left, device_id_type=MESH)
    )
    for step in range(1, ops.cols):
        peer = lax.rem(ops.col + step, ops.cols)
        pl.semaphore_signal(barrier, inc=1, device_id=(ops.row, peer), device_id_type=MESH)
    for level in levels:
        level.clear_ends()
    for copy in early:
        copy.wait()
    for b in fine.edges():
        fine.make_diagonal(b)
        fine.start_block(b)
    pl.semaphore_wait(
        barrier, ops.cols - 1 + next_row.astype(jnp.int32) + previous_row.astype(jnp.int32)
    )

    def middle_diagonal(b):
        fine.make_diagonal(b)

    fine.ops.start(fine.halo_copies(0))
    middle.wait()

    def inner_start(b):
        fine.make_diagonal(b)
        fine.start_block(b)

    loop(*fine.inner(), inner_start)
    for copy in later:
        copy.wait()
    loop(0, fine.n // 2, fine.make_onehot, 1)
    fine.apply(0, fine.first_sweep)
    fine.ops.start(fine.halo_copies(1))
    loop(fine.n // 2, fine.n, fine.make_onehot, 1)
    for level in (second, third):
        loop(0, level.n, level.make_onehot, 1)
        loop(0, level.n, level.make_diagonal, 4)
    fine.apply(1, fine.residual)

    def into_level(level):
        def into(block, value):
            level.ref["f"][block] = value

        return into

    fine.restrict(into_level(second))
    for level, following in ((second, third), (third, None)):
        for b in level.edges():
            level.start_block(b)
        if following is not None:
            level.down(into_level(following))
        else:

            def into_coarse(block, value):
                gathered[ops.col] = value.astype(BF16)

            level.down(into_coarse)

    sends = []
    for step in range(1, ops.cols):
        peer = lax.rem(ops.col + step, ops.cols)
        copy = pltpu.make_async_remote_copy(
            gathered.at[ops.col], gathered.at[ops.col],
            gather_send.at[step - 1], gather_recv.at[step - 1],
            device_id=(ops.row, peer), device_id_type=MESH,
        )
        copy.start()
        sends.append(copy)
    for step in range(1, ops.cols):
        source = lax.rem(ops.col + ops.cols - step, ops.cols)
        pltpu.make_async_remote_copy(
            gathered.at[source], gathered.at[source],
            gather_send.at[step - 1], gather_recv.at[step - 1],
            device_id=(ops.row, source), device_id_type=MESH,
        ).wait_recv()
    everything = jnp.concatenate([gathered[p] for p in range(ops.cols)], axis=1)
    solved = lax.dot_general(
        everything, inverse[...], (((1,), (1,)), ((), ())), preferred_element_type=F32
    )
    third.ref["uout"][...] = solved.astype(BF16)

    def into_coarse_vector(level):
        def put(b, x):
            level.ref["uout"][:, b * bs : (b + 1) * bs] = x.astype(BF16)

        return put

    third.up(into_coarse_vector(second))
    second.up(into_coarse_vector(fine))

    def put_out(b, x):
        out[b] = x

    fine.up(put_out)
    result = pltpu.make_async_copy(out, out_hbm, out_sem.at[0])
    result.start()
    for level in levels:
        level.drain()
    for copy in sends:
        copy.wait_send()
    result.wait()


def on_device(
    right_sides,
    weights_fine, columns_fine, degree_fine, owners_fine, slots_fine,
    weights_second, columns_second, degree_second, owners_second, slots_second,
    weights_third, columns_third, degree_third, owners_third, slots_third,
    coarse_inverse,
):
    n0, r, bs = right_sides.shape
    n1, n2 = weights_second.shape[0], weights_third.shape[0]
    k = weights_fine.shape[1]
    c3, m3 = coarse_inverse.shape
    cols = lax.axis_size("col")
    sizes = ((n0, n1 * bs), (n1, n2 * bs), (n2, c3))
    merged = lambda w: w.reshape(w.shape[0], k * bs, bs)
    args = [right_sides, coarse_inverse]
    specs = [pl.BlockSpec(memory_space=pl.ANY)] * 2
    for w, c, d, o, s in (
        (weights_fine, columns_fine, degree_fine, owners_fine, slots_fine),
        (weights_second, columns_second, degree_second, owners_second, slots_second),
        (weights_third, columns_third, degree_third, owners_third, slots_third),
    ):
        args += [c, merged(w), d, o, s]
        specs += [pl.BlockSpec(memory_space=pltpu.SMEM)]
        specs += [pl.BlockSpec(memory_space=pl.ANY)] * 4
    scratch = []
    for n, t in sizes:
        scratch += [
            pltpu.VMEM((n, k * bs, bs), BF16),
            pltpu.VMEM((n, bs), F32),
            pltpu.VMEM((n, bs), jnp.int32),
            pltpu.VMEM((n, bs), jnp.int32),
            pltpu.VMEM((n, 8, bs), F32),
            pltpu.VMEM((n, 8, bs), F32),
            pltpu.VMEM((n, r, bs), F32),
            pltpu.VMEM((4, n, r, bs), BF16),
            *[pltpu.VMEM((6, r, bs), BF16)] * 8,
            pltpu.VMEM(((4 if SPLIT_OWN else 3) * r, n * bs), BF16),
            pltpu.VMEM((t, n * bs), BF16),
            pltpu.VMEM((2, r, t), BF16),
            pltpu.VMEM((2, r, t), BF16),
            pltpu.VMEM((r, t), F32),
            pltpu.VMEM((r, t), BF16),
            pltpu.VMEM((2, r, t), BF16),
        ]
    scratch += [
        pltpu.VMEM((n0, r, bs), BF16),
        pltpu.VMEM((n1, r, bs), F32),
        pltpu.VMEM((n2, r, bs), F32),
        pltpu.VMEM((c3, m3), BF16),
        pltpu.VMEM((cols, r, c3), BF16),
        pltpu.VMEM((n0, r, bs), F32),
        pltpu.SemaphoreType.DMA((18, 2)),
        pltpu.SemaphoreType.DMA((18, 2)),
        pltpu.SemaphoreType.DMA((cols,)),
        pltpu.SemaphoreType.DMA((cols,)),
        pltpu.SemaphoreType.DMA((24,)),
        pltpu.SemaphoreType.DMA((1,)),
    ]
    return pl.pallas_call(
        functools.partial(kernel, sizes, r, bs, k, m3),
        out_shape=jax.ShapeDtypeStruct((n0, r, bs), F32),
        in_specs=specs,
        out_specs=pl.BlockSpec(memory_space=pl.ANY),
        scratch_shapes=scratch,
        compiler_params=pltpu.CompilerParams(
            collective_id=0, has_side_effects=True, vmem_limit_bytes=48 * 1024 * 1024
        ),
        name="vcycle",
    )(*args)


def solution(mesh):
    whole = ("row", "col")
    vector, matrix, table = P(whole, None, None), P(whole, None, None, None), P(whole, None)
    level = (matrix, table, table, table, table)
    return jax.shard_map(
        on_device,
        mesh=mesh,
        in_specs=(vector, *level, *level, *level, table),
        out_specs=vector,
        check_vma=False,
    )
```

time: 336 us -> 119 us (0.35)
  starting transfers between devices: 166 us -> 0 us
  Pallas kernels: 0 us -> 103 us
  other arithmetic: 40.2 us -> 0 us
  waiting for transfers between devices: 34.9 us -> 0 us
  blocking collectives: 30.8 us -> 0 us
  local copies, waits for them, and re-layouts: 43.6 us -> 15.4 us
  matrix products: 16.8 us -> 0 us
    ppermute x36 -> x0, starting transfers between devices: 166 us -> none  [the longest x15 107 us: extended_2(): lax.ppermute(lax.slice_in_dim(block, 0, width, axis=dim), axis, backward)]
    pallas_call x0 -> x1, Pallas kernels: none -> 103 us  [on_device(): pl.pallas_call(functools.partial(kernel, sizes, r, bs, k, m3), out_shape=...]
    gather x15 -> x0, local copies, waits for them, and re-layouts: 34.9 us -> none  [the longest x3 17.7 us: prolong(): return current_iterate + make_blocks(extended[targets])]
    ppermute x36 -> x0, waiting for transfers between devices: 34.9 us -> none  [the longest x15 23.1 us: extended_2(): lax.ppermute(lax.slice_in_dim(block, 0, width, axis=dim), axis, backward)]
    scatter-add x3 -> x0, other arithmetic: 30.8 us -> none  [restrict(): jax.ops.segment_sum(gather_rows(residual), targets, num_segments=3 * coar...]
    all_gather x1 -> x0, blocking collectives: 30.8 us -> none  [coarse_solve(): lax.all_gather(rounded, 'col', axis=1, tiled=True)]
    dot_general x13 -> x0, matrix products: 16.8 us -> none  [the longest x12 16.5 us: apply_operator(): jnp.einsum('nkrb,nkbc->nrc', picked, weights, preferred_element_type=jnp....]
    unnamed x44 -> x33, local copies, waits for them, and re-layouts: 0.91 us -> 15.4 us
  transfers between devices with their start and end apart: 36 -> 0, of which waited for: 20 -> 0; matrix products, arithmetic and copies ran while one was open for 0% -> 0% of each run, Pallas kernels for 0% -> 0%
where the time goes in v1:
time: 119 us; the launch traced here: 118 us
  Pallas kernels  103 us (87%)
  local copies, waits for them, and re-layouts  15.4 us (13%)
    pallas_call x1, Pallas kernels, on_device(): pl.pallas_call(functools.partial(kernel, sizes, r, bs, k, m3), out_shape=...  103 us
    unnamed x33, local copies, waits for them, and re-layouts  15.4 us

profile of v1, /device:TPU:2, one launch (start us, length us, event | category | flops | bytes accessed | tf_op | source)
XLA Modules:
  0.0 118.1 jit_solution(12497016033457226285)
XLA Ops:
  0.0 0.8 copy.19.refs_7_
  0.8 0.8 copy.18.refs_2_
  1.5 0.0 copy-start
  1.5 1.9 %copy-done = bf16[32,3,128,128]{3,2,1,0:T(8,128)(2,1)S(1)} copy-done((bf16[32,3,128,128]{3,2,1,0:T(8,128)(2,1)S(1)}, bf16[32,3,128,128]{3,2,1,0:T(8,128)(2,1)}, u32[]{:S(2)}) %copy-start) | copy-done | bytes 3145752
  3.4 0.0 copy-start.1
  3.4 1.1 copy-done.1
  4.5 0.0 copy-start.2
  4.5 1.0 copy-done.2
  5.6 0.0 copy-start.3
  5.6 0.9 copy-done.3
  6.5 0.0 copy-start.4
  6.5 0.9 copy-done.4
  7.5 0.0 copy-start.5
  7.5 0.7 copy-done.5
  8.2 0.0 copy-start.6
  8.2 0.7 copy-done.6
  8.9 0.0 copy-start.7
  8.9 0.7 copy-done.7
  9.6 0.0 copy-start.8
  9.6 0.7 copy-done.8
  10.3 0.0 copy-start.9
  10.3 0.7 copy-done.9
  11.0 0.0 copy-start.10
  11.0 0.7 copy-done.10
  11.7 0.0 copy-start.11
  11.7 0.7 copy-done.11
  12.4 0.0 copy-start.12
  12.4 0.7 copy-done.12
  13.0 0.0 copy-start.13
  13.0 0.7 copy-done.13
  13.7 0.0 copy-start.14
  13.7 0.7 copy-done.14
  14.4 102.7 %vcycle.1 = f32[32,64,128]{2,1,0:T(8,128)S(1)} custom-call(bf16[32,64,128]{2,1,0:T(8,128)(2,1)S(1)} %copy-done.2, bf16[128,1024]{1,0:T(8,128)(2,1)S(1)} %copy-done.3, s32[32,3]{1,0:T(8,128)S(1)} %copy.18.refs_2_, bf16[32,384,128]{2,1,0:T(8,128)(2,1)S(1)} %bitcast.3, f32[32,128]{1,0:T(8,128)S(1)} %copy-done.5, s32[32,128]{1,0:T(8,128)S(1)} %copy-done.6, ...), custom_call_target="tpu_custom_call" | custom-call | tf_op jit(solution)/shard_map/vcycle/pallas_call | solution.py:541
  117.1 1.0 copy.21
Async XLA Ops:
  1.5 1.9 %copy-start = (bf16[32,3,128,128]{3,2,1,0:T(8,128)(2,1)S(1)}, bf16[32,3,128,128]{3,2,1,0:T(8,128)(2,1)}, u32[]{:S(2)}) copy-start(bf16[32,3,128,128]{3,2,1,0:T(8,128)(2,1)} %param.18) | copy-start | bytes 9437188
  3.4 1.1 copy-start.1
  4.5 1.0 copy-start.2
  5.6 0.9 copy-start.3
  6.5 0.9 copy-start.4
  7.5 0.7 copy-start.5
  8.2 0.7 copy-start.6
  8.9 0.7 copy-start.7
  9.6 0.7 copy-start.8
  10.3 0.7 copy-start.9
  11.0 0.7 copy-start.10
  11.7 0.7 copy-start.11
  12.4 0.7 copy-start.12
  13.0 0.7 copy-start.13
  13.7 0.7 copy-start.14

commit v2 on v1

--- a/solution.py
+++ b/solution.py
@@ -29,6 +29,29 @@
     def step(outer, carry):
         for inner in range(unroll):
             body(low + outer * unroll + inner)
+        return carry
+
+    lax.fori_loop(0, count // unroll, step, 0)
+
+
+def grouped(low, high, first, then, unroll=7):
+    count = high - low
+    if count <= 0:
+        return
+    while count % unroll:
+        unroll -= 1
+
+    def group(start):
+        made = [first(start + inner) for inner in range(unroll)]
+        for inner in range(unroll):
+            then(start + inner, made[inner])
+
+    if count == unroll:
+        group(low)
+        return
+
+    def step(outer, carry):
+        group(low + outer * unroll)
         return carry
 
     lax.fori_loop(0, count // unroll, step, 0)
@@ -51,9 +74,11 @@
     def inner(self):
         return (0, 0) if self.single else (2, self.n - 2)
 
-    def make_diagonal(self, b):
+    def weight_sums(self, b):
         w = self.ref["w"][b]
-        total = jnp.dot(jnp.ones((8, w.shape[0]), BF16), w, preferred_element_type=F32)
+        return jnp.dot(jnp.ones((8, w.shape[0]), BF16), w, preferred_element_type=F32)
+
+    def put_diagonal(self, b, total):
         degree = self.ref["deg"][pl.ds(b, 1), :]
         g = degree + total * self.scale
         self.ref["g"][b] = g
@@ -68,7 +93,7 @@
 
     def product(self, i, b, where):
         if where == "inner":
-            buf, offset = self.ref["vb"].at[i], self.base
+            buf, offset = self.ref[f"vb{i}"], self.base
         elif where == "low":
             buf, offset = self.ref[f"lo{i}"], self.base - 2
         else:
@@ -81,7 +106,7 @@
         return jnp.dot(left, self.ref["w"][b], preferred_element_type=F32) * self.scale
 
     def halo_copies(self, i):
-        n, ops, vb = self.n, self.ops, self.ref["vb"].at[i]
+        n, ops, vb = self.n, self.ops, self.ref[f"vb{i}"]
         if self.single:
             low_dst, high_dst = self.ref[f"lo{i}"].at[0:2], self.ref[f"lo{i}"].at[4:6]
         else:
@@ -91,33 +116,34 @@
     def fill_edges(self, i):
         n = self.n
         if self.single:
-            self.ref[f"lo{i}"][2:4] = self.ref["vb"][i, 0:2]
+            self.ref[f"lo{i}"][2:4] = self.ref[f"vb{i}"][0:2]
         else:
-            self.ref[f"lo{i}"][2:6] = self.ref["vb"][i, 0:4]
-            self.ref[f"hi{i}"][0:4] = self.ref["vb"][i, n - 4 : n]
-
-    def run_edges(self, body):
-        for b in self.edges():
-            body(b, "low" if b < 2 else "high")
+            self.ref[f"lo{i}"][2:6] = self.ref[f"vb{i}"][0:4]
+            self.ref[f"hi{i}"][0:4] = self.ref[f"vb{i}"][n - 4 : n]
+
+    def run_edges(self, i, body):
+        made = [self.product(i, b, "low" if b < 2 else "high") for b in self.edges()]
+        for b, product in zip(self.edges(), made):
+            body(b, product)
 
     def apply(self, i, body):
-        loop(*self.inner(), lambda b: body(b, "inner"))
+        grouped(*self.inner(), lambda b: self.product(i, b, "inner"), body)
         self.fill_edges(i)
         self.ops.wait(self.halo_copies(i))
-        self.run_edges(body)
+        self.run_edges(i, body)
 
     def start_block(self, b):
-        self.ref["vb"][0, b] = (self.row("gi", b) * self.f(b)).astype(BF16)
-
-    def first_sweep(self, b, where):
+        self.ref["vb0"][b] = (self.row("gi", b) * self.f(b)).astype(BF16)
+
+    def first_sweep(self, b, product):
         f, gi = self.f(b), self.row("gi", b)
         x0 = gi * f
-        x = (1.0 - DAMPING) * x0 + gi * (f + self.product(0, b, where))
+        x = (1.0 - DAMPING) * x0 + gi * (f + product)
         self.ref["x"][b] = x
-        self.ref["vb"][1, b] = x.astype(BF16)
-
-    def residual(self, b, where):
-        res = self.f(b) - self.row("g", b) * self.ref["x"][b] + self.product(1, b, where)
+        self.ref["vb1"][b] = x.astype(BF16)
+
+    def residual(self, b, product):
+        res = self.f(b) - self.row("g", b) * self.ref["x"][b] + product
         rel = self.owner(b)
         columns = pl.ds(pl.multiple_of(b * self.bs, self.bs), self.bs)
         rows = self.r
@@ -209,21 +235,25 @@
     def pair_columns(self, pair):
         return pl.ds(pl.multiple_of(pair * 2 * self.bs, 2 * self.bs), 2 * self.bs)
 
-    def add_own(self, pair):
-        value = jnp.dot(
+    def own_part(self, pair):
+        return jnp.dot(
             self.ref["uout"][...], self.ref["oh"][:, self.pair_columns(pair)],
             preferred_element_type=F32,
         )
+
+    def add_own(self, pair, value):
         for half in range(2):
             b = 2 * pair + half
             part = value[:, half * self.bs : (half + 1) * self.bs]
             self.ref["x"][b] = self.ref["x"][b] + jnp.where(self.owner(b) == 0, part, 0.0)
 
-    def add_others(self, pair):
+    def others_part(self, pair):
         left = jnp.concatenate([self.ref["uin"][0], self.ref["uin"][1]], axis=0)
-        value = jnp.dot(
+        return jnp.dot(
             left, self.ref["oh"][:, self.pair_columns(pair)], preferred_element_type=F32
         )
+
+    def add_others(self, pair, value):
         for half in range(2):
             b = 2 * pair + half
             at = slice(half * self.bs, (half + 1) * self.bs)
@@ -232,15 +262,15 @@
             x = x + jnp.where(rel < 0, value[0 : self.r, at], 0.0)
             x = x + jnp.where(rel > 0, value[self.r : 2 * self.r, at], 0.0)
             self.ref["x"][b] = x
-            self.ref["vb"][2, b] = x.astype(BF16)
+            self.ref["vb2"][b] = x.astype(BF16)
 
     def sweep(self, i, last, out=None):
-        def body(b, where):
+        def body(b, product):
             gi = self.row("gi", b)
-            x = (1.0 - DAMPING) * self.ref["x"][b] + gi * (self.f(b) + self.product(i, b, where))
+            x = (1.0 - DAMPING) * self.ref["x"][b] + gi * (self.f(b) + product)
             self.ref["x"][b] = x
             if not last:
-                self.ref["vb"][i + 1, b] = x.astype(BF16)
+                self.ref[f"vb{i + 1}"][b] = x.astype(BF16)
             elif out is not None:
                 out(b, x)
 
@@ -250,14 +280,15 @@
         copies = self.prolong_copies()
         self.ops.start(copies)
         pairs = self.n // 2
-        loop(0, pairs, self.add_own, 2)
+        grouped(0, pairs, self.own_part, self.add_own, 2)
         self.ops.wait(copies)
-        self.add_others(0)
-        if not self.single:
-            self.add_others(pairs - 1)
+        ends = [0] if self.single else [0, pairs - 1]
+        made = [self.others_part(pair) for pair in ends]
+        for pair, value in zip(ends, made):
+            self.add_others(pair, value)
         self.ops.start(self.halo_copies(2))
         if not self.single:
-            loop(1, pairs - 1, self.add_others, 2)
+            grouped(1, pairs - 1, self.others_part, self.add_others, 2)
         self.apply(2, self.sweep(2, False))
         self.ops.start(self.halo_copies(3))
         self.apply(3, self.sweep(3, True, out))
@@ -321,7 +352,7 @@
 
 LEVEL_HBM = ("w", "deg", "own", "slot")
 LEVEL_SCRATCH = (
-    "w", "deg", "own", "slot", "g", "gi", "x", "vb",
+    "w", "deg", "own", "slot", "g", "gi", "x", "vb0", "vb1", "vb2", "vb3",
     "lo0", "lo1", "lo2", "lo3", "hi0", "hi1", "hi2", "hi3", "res", "oh",
     "rout", "rin", "rown", "uout", "uin",
 )
@@ -387,24 +418,21 @@
         level.clear_ends()
     for copy in early:
         copy.wait()
-    for b in fine.edges():
-        fine.make_diagonal(b)
+    def diagonal_and_start(b, total):
+        fine.put_diagonal(b, total)
         fine.start_block(b)
+
+    made = [fine.weight_sums(b) for b in fine.edges()]
+    for b, total in zip(fine.edges(), made):
+        diagonal_and_start(b, total)
     pl.semaphore_wait(
         barrier, ops.cols - 1 + next_row.astype(jnp.int32) + previous_row.astype(jnp.int32)
     )
 
-    def middle_diagonal(b):
-        fine.make_diagonal(b)
-
     fine.ops.start(fine.halo_copies(0))
     middle.wait()
 
-    def inner_start(b):
-        fine.make_diagonal(b)
-        fine.start_block(b)
-
-    loop(*fine.inner(), inner_start)
+    grouped(*fine.inner(), fine.weight_sums, diagonal_and_start)
     for copy in later:
         copy.wait()
     loop(0, fine.n // 2, fine.make_onehot, 1)
@@ -413,7 +441,7 @@
     loop(fine.n // 2, fine.n, fine.make_onehot, 1)
     for level in (second, third):
         loop(0, level.n, level.make_onehot, 1)
-        loop(0, level.n, level.make_diagonal, 4)
+        grouped(0, level.n, level.weight_sums, level.put_diagonal, 8)
     fine.apply(1, fine.residual)
 
     def into_level(level):
@@ -514,7 +542,7 @@
             pltpu.VMEM((n, 8, bs), F32),
             pltpu.VMEM((n, 8, bs), F32),
             pltpu.VMEM((n, r, bs), F32),
-            pltpu.VMEM((4, n, r, bs), BF16),
+            *[pltpu.VMEM((n, r, bs), BF16)] * 4,
             *[pltpu.VMEM((6, r, bs), BF16)] * 8,
             pltpu.VMEM(((4 if SPLIT_OWN else 3) * r, n * bs), BF16),
             pltpu.VMEM((t, n * bs), BF16),

time: 119 us -> 113 us (0.950)
  Pallas kernels: 103 us -> 96.7 us
    pallas_call x1, Pallas kernels: 103 us -> 96.7 us  [on_device(): pl.pallas_call(functools.partial(kernel, sizes, r, bs, k, m3), out_shape=...]
where the time goes in v2:
time: 113 us; the launch traced here: 112 us
  Pallas kernels  96.7 us (86%)
  local copies, waits for them, and re-layouts  15.4 us (14%)
    pallas_call x1, Pallas kernels, on_device(): pl.pallas_call(functools.partial(kernel, sizes, r, bs, k, m3), out_shape=...  96.7 us
    unnamed x33, local copies, waits for them, and re-layouts  15.4 us

profile of v2, /device:TPU:2, one launch (start us, length us, event | category | flops | bytes accessed | tf_op | source)
XLA Modules:
  0.0 112.1 jit_solution(3213295669926479480)
XLA Ops:
  0.0 0.8 copy.19.refs_7_
  0.8 0.8 copy.18.refs_2_
  1.5 0.0 copy-start
  1.5 1.9 %copy-done = bf16[32,3,128,128]{3,2,1,0:T(8,128)(2,1)S(1)} copy-done((bf16[32,3,128,128]{3,2,1,0:T(8,128)(2,1)S(1)}, bf16[32,3,128,128]{3,2,1,0:T(8,128)(2,1)}, u32[]{:S(2)}) %copy-start) | copy-done | bytes 3145752
  3.4 0.0 copy-start.1
  3.4 1.1 %copy-done.1 = bf16[8,3,128,128]{3,2,1,0:T(8,128)(2,1)S(1)} copy-done((bf16[8,3,128,128]{3,2,1,0:T(8,128)(2,1)S(1)}, bf16[8,3,128,128]{3,2,1,0:T(8,128)(2,1)}, u32[]{:S(2)}) %copy-start.1) | copy-done | bytes 786456
  4.5 0.0 copy-start.2
  4.5 1.0 copy-done.2
  5.6 0.0 copy-start.3
  5.6 0.9 copy-done.3
  6.5 0.0 copy-start.4
  6.5 0.9 copy-done.4
  7.5 0.0 copy-start.5
  7.5 0.7 copy-done.5
  8.2 0.0 copy-start.6
  8.2 0.7 copy-done.6
  8.9 0.0 copy-start.7
  8.9 0.7 copy-done.7
  9.6 0.0 copy-start.8
  9.6 0.7 copy-done.8
  10.3 0.0 copy-start.9
  10.3 0.7 copy-done.9
  11.0 0.0 copy-start.10
  11.0 0.7 copy-done.10
  11.7 0.0 copy-start.11
  11.7 0.7 copy-done.11
  12.4 0.0 copy-start.12
  12.4 0.7 copy-done.12
  13.0 0.0 copy-start.13
  13.0 0.7 copy-done.13
  13.7 0.0 copy-start.14
  13.7 0.7 copy-done.14
  14.4 96.7 %vcycle.1 = f32[32,64,128]{2,1,0:T(8,128)S(1)} custom-call(bf16[32,64,128]{2,1,0:T(8,128)(2,1)S(1)} %copy-done.2, bf16[128,1024]{1,0:T(8,128)(2,1)S(1)} %copy-done.3, s32[32,3]{1,0:T(8,128)S(1)} %copy.18.refs_2_, bf16[32,384,128]{2,1,0:T(8,128)(2,1)S(1)} %bitcast.3, f32[32,128]{1,0:T(8,128)S(1)} %copy-done.5, s32[32,128]{1,0:T(8,128)S(1)} %copy-done.6, ...), custom_call_target="tpu_custom_call" | custom-call | tf_op jit(solution)/shard_map/vcycle/pallas_call | solution.py:569
  111.1 1.0 copy.21
Async XLA Ops:
  1.5 1.9 %copy-start = (bf16[32,3,128,128]{3,2,1,0:T(8,128)(2,1)S(1)}, bf16[32,3,128,128]{3,2,1,0:T(8,128)(2,1)}, u32[]{:S(2)}) copy-start(bf16[32,3,128,128]{3,2,1,0:T(8,128)(2,1)} %param.18) | copy-start | bytes 9437188
  3.4 1.1 %copy-start.1 = (bf16[8,3,128,128]{3,2,1,0:T(8,128)(2,1)S(1)}, bf16[8,3,128,128]{3,2,1,0:T(8,128)(2,1)}, u32[]{:S(2)}) copy-start(bf16[8,3,128,128]{3,2,1,0:T(8,128)(2,1)} %param.23) | copy-start | bytes 2359300
  4.5 1.0 copy-start.2
  5.6 0.9 copy-start.3
  6.5 0.9 copy-start.4
  7.5 0.7 copy-start.5
  8.2 0.7 copy-start.6
  8.9 0.7 copy-start.7
  9.6 0.7 copy-start.8
  10.3 0.7 copy-start.9
  11.0 0.7 copy-start.10
  11.7 0.7 copy-start.11
  12.4 0.7 copy-start.12
  13.0 0.7 copy-start.13
  13.7 0.7 copy-start.14
